TPU v7x, 128 devices: a whole 4x4x4 slice. The times are simulated.
128 devices in a mesh: cp: 8 (over z, y_lo), tp: 16 (over x, y_hi, core).
Axes of the slice: x: 4, y: 4 (y_hi: 2, y_lo: 2; y = y_hi * 2 + y_lo), z: 4, core: 2. Of those that a mesh axis runs over, the one named last changes fastest.
Arguments:
- checkpoint: bfloat16 [4096, 8192], P('cp', 'tp'), may hold values from -6 to 6
- norm_gain: float32 [8192], replicated, may hold values from 0.1 to 1.9
- query_weight: bfloat16 [8192, 8192], P(None, 'tp'), may hold values from -4 to 4
- key_weight: bfloat16 [8192, 1024], P(None, 'tp'), may hold values from -1 to 1
- value_weight: bfloat16 [8192, 1024], P(None, 'tp'), may hold values from -0.0625 to 0.0625
- output_weight: bfloat16 [8192, 8192], P('tp'), may hold values from -0.09375 to 0.09375
- block_order: int32 [16], replicated, may hold values from 0 to 15, each once
Outputs:
- projected: bfloat16 [4096, 8192], P('cp', 'tp')
- log_normalizer: float32 [64, 4096], P('tp', 'cp')
Inputs may be any that keep to these rules, and one draw needn't show every extreme that they name: `block_order`: each of 0 to 15 once.
All inputs are finite; a program needn't handle non-finite values.
Results may differ from a plain program's by a relative error of at most 0.019.
Values may be sent and summed in bfloat16 or wider, within the bound.
A program may use at most 128 MiB of HBM per device.

v0:
```python
import math

import jax
import jax.numpy as jnp
from jax import lax
from jax.sharding import PartitionSpec as P

KV_HEADS = 8
HEAD_DIM = 128


rope_base = 500000.0
norm_epsilon = 1e-05
masked_score = -1e30


def partner_2(block, axis, stride):
    count = lax.axis_size(axis)
    route = []
    for low in range(count):
        high = low | 1 << stride
        if high != low and high < count:
            route += [(low, high), (high, low)]
    return lax.ppermute(block, axis, route)


def from_behind(block, axis, distance):
    devices = range(lax.axis_size(axis))
    route = [((i - distance) % len(devices), i) for i in devices]
    return lax.ppermute(block, axis, route)


def turn_pairs(matrix, positions, first_pair):
    pair_count = matrix.shape[-1] // 2
    pair_index = (first_pair + jnp.arange(pair_count, dtype=jnp.int32)).astype(jnp.float32)
    inverse_rates = rope_base ** (-2.0 * pair_index / HEAD_DIM)
    angles = positions.astype(jnp.float32)[:, None] * inverse_rates[None, :]
    cosine = jnp.cos(angles)[:, None, :]
    sine_part = jnp.sin(angles)[:, None, :]
    paired = matrix.reshape(matrix.shape[0], matrix.shape[1], pair_count, 2)
    former = paired[..., 0]
    latter = paired[..., 1]
    turned = jnp.stack(
        [former * cosine - latter * sine_part, former * sine_part + latter * cosine], axis=-1
    )
    return turned.reshape(matrix.shape)


def shards(
    checkpoint, norm_gain, query_weight, key_weight, value_weight, output_weight, block_order
):
    tok_rows = checkpoint.shape[0]
    block_rows = tok_rows // 2
    local_heads = query_weight.shape[1] // HEAD_DIM
    key_columns = key_weight.shape[1]
    context_rank = lax.axis_index("cp")
    tensor_rank = lax.axis_index("tp")
    row_offsets = jnp.arange(block_rows, dtype=jnp.int32)
    own_blocks = lax.dynamic_slice_in_dim(block_order, 2 * context_rank, 2)
    own_positions = (own_blocks[:, None] * block_rows + row_offsets[None, :]).reshape(tok_rows)
    gathered = lax.all_gather(checkpoint, "tp", axis=1, tiled=True)
    widened = gathered.astype(jnp.float32)
    mean_square = jnp.mean(widened * widened, axis=-1, keepdims=True)
    normed = (widened * lax.rsqrt(mean_square + norm_epsilon) * norm_gain).astype(jnp.bfloat16)
    query_features = jnp.dot(normed, query_weight, preferred_element_type=jnp.float32)
    key_features = jnp.dot(normed, key_weight, preferred_element_type=jnp.float32)
    value_features = jnp.dot(normed, value_weight, preferred_element_type=jnp.float32)
    queries = turn_pairs(
        query_features.reshape(tok_rows, local_heads, HEAD_DIM), own_positions, 0
    ).astype(jnp.bfloat16)
    sharing = lax.axis_size("tp") // KV_HEADS
    part_of_head = tensor_rank % sharing
    key_part = turn_pairs(
        key_features.reshape(tok_rows, 1, key_columns),
        own_positions,
        part_of_head * (key_columns // 2),
    )
    key_part = key_part.astype(jnp.bfloat16).reshape(tok_rows, key_columns)
    value_part = value_features.astype(jnp.bfloat16)
    own_pair = jnp.stack([key_part, value_part])
    partner = partner_2(own_pair, "tp", 0)
    lower_first = jnp.concatenate([own_pair, partner], axis=-1)
    upper_first = jnp.concatenate([partner, own_pair], axis=-1)
    key_value = jnp.where(part_of_head == 0, lower_first, upper_first)
    score_scale = 1.0 / math.sqrt(HEAD_DIM)

    def absorb(running, query_slot, key_block, key_rows, value_rows):
        query_block = own_blocks[query_slot]
        top_scores, totals, weighted = running
        query_rows = queries[query_slot * block_rows : (query_slot + 1) * block_rows]
        scores = (
            jnp.einsum("qhd,kd->qhk", query_rows, key_rows, preferred_element_type=jnp.float32)
            * score_scale
        )
        query_places = query_block * block_rows + row_offsets
        key_places = key_block * block_rows + row_offsets
        allowed = (key_places[None, :] <= query_places[:, None])[:, None, :]
        scores = jnp.where(allowed, scores, masked_score)
        old_top = top_scores[query_slot]
        new_top = jnp.maximum(old_top, jnp.max(scores, axis=-1))
        weights = jnp.where(allowed, jnp.exp(scores - new_top[..., None]), 0.0)
        shrink = jnp.exp(old_top - new_top)
        new_total = totals[query_slot] * shrink + jnp.sum(weights, axis=-1)
        new_sum = weighted[query_slot] * shrink[..., None] + jnp.einsum(
            "qhk,kd->qhd",
            weights.astype(jnp.bfloat16),
            value_rows,
            preferred_element_type=jnp.float32,
        )
        return (
            top_scores.at[query_slot].set(new_top),
            totals.at[query_slot].set(new_total),
            weighted.at[query_slot].set(new_sum),
        )

    def visit_rows(running, key_value_rows, first_row):
        block_count = key_value_rows.shape[1] // block_rows

        def one_block(block_index, current):
            rows_here = lax.dynamic_slice_in_dim(
                key_value_rows, block_index * block_rows, block_rows, 1
            )
            stored = first_row // block_rows + block_index
            key_block = lax.dynamic_index_in_dim(block_order, stored, 0, keepdims=False)
            for query_slot in range(2):
                current = absorb(current, query_slot, key_block, rows_here[0], rows_here[1])
            return current

        return lax.fori_loop(0, block_count, one_block, running)

    running = (
        jnp.full((2, block_rows, local_heads), masked_score, jnp.float32),
        jnp.zeros((2, block_rows, local_heads), jnp.float32),
        jnp.zeros((2, block_rows, local_heads, HEAD_DIM), jnp.float32),
    )
    running = visit_rows(running, key_value, context_rank * tok_rows)
    context_size = lax.axis_size("cp")

    def pass_turn(turn_index, carried):
        current, travelling = carried
        travelling = from_behind(travelling, "cp", 1)
        source = (context_rank - turn_index) % context_size
        return (visit_rows(current, travelling, source * tok_rows), travelling)

    running, unused = lax.fori_loop(1, context_size, pass_turn, (running, key_value))
    top_scores, totals, weighted = running
    attended = (
        (weighted / totals[..., None])
        .astype(jnp.bfloat16)
        .reshape(tok_rows, local_heads * HEAD_DIM)
    )
    normalizer = jnp.transpose((top_scores + jnp.log(totals)).reshape(tok_rows, local_heads))
    partial_terms = jnp.dot(attended, output_weight, preferred_element_type=jnp.float32)
    projected = lax.psum_scatter(
        partial_terms.astype(jnp.bfloat16), "tp", scatter_dimension=1, tiled=True
    )
    return (projected, normalizer)


def solution(mesh):
    return jax.shard_map(
        shards,
        mesh=mesh,
        in_specs=(
            P("cp", "tp"),
            P(),
            P(None, "tp"),
            P(None, "tp"),
            P(None, "tp"),
            P("tp", None),
            P(),
        ),
        out_specs=(P("cp", "tp"), P("tp", "cp")),
        check_vma=False,
    )
```

profile of v0, /device:TPU:1, one launch (start us, length us, event | category | flops | bytes accessed | tf_op | source)
XLA Modules:
  0.0 365.8 jit_solution(13176178506513169410)
XLA Ops:
  7.2 0.7 all-gather.2.cloned.1.call-update
  8.0 0.7 broadcast_multiply_fusion
  8.7 0.6 fusion.101
  10.8 0.5 multiply_cosine_fusion
  11.3 81.6 %all-gather.2.cloned.1.call-done = bf16[512,8192]{1,0:T(8,128)(2,1)} async-done(((bf16[512,512]{1,0:T(8,128)(2,1)}), bf16[512,8192]{1,0:T(8,128)(2,1)}) %all-gather.2.cloned.1.call-update) | async-done | bytes 8388624 | tf_op jit(solution)/shard_map/all_gather | solution.py:61
  92.9 5.1 %fusion.76 = f32[512]{0:T(512)S(1)} fusion(bf16[512,8192]{1,0:T(8,128)(2,1)} %all-gather.2.cloned.1.call-done), kind=kLoop, calls=%fused_computation.118 | loop fusion | flops 12582400 | bytes 8390656 | tf_op jit(solution)/shard_map/reduce_sum | solution.py:63
  98.1 11.6 %fusion.90 = f32[512,512]{0,1:T(8,128)S(1)} fusion(bf16[8192,512]{1,0:T(8,128)(2,1)} %param.39, bf16[512,8192]{1,0:T(8,128)(2,1)} %all-gather.2.cloned.1.call-done, f32[8192]{0:T(1024)S(1)} %copy-done.2, f32[512]{0:T(512)S(1)} %add_rsqrt_fusion), kind=kOutput, calls=%fused_computation.151 | convolution fusion | flops 4311744512 | bytes 17860608 | tf_op jit(solution)/shard_map/dot_general | solution.py:65
  109.6 0.6 reshape_reshape.7
  110.3 6.1 %fusion.93 = f32[512,64]{0,1:T(8,128)S(1)} fusion(bf16[8192,64]{0,1:T(8,128)(2,1)S(1)} %copy-done, bf16[512,8192]{1,0:T(8,128)(2,1)} %all-gather.2.cloned.1.call-done, f32[8192]{0:T(1024)S(1)} %copy-done.2, f32[512]{0:T(512)S(1)} %add_rsqrt_fusion), kind=kOutput, calls=%fused_computation.152 | convolution fusion | flops 553648128 | bytes 9603072 | tf_op jit(solution)/shard_map/dot_general | solution.py:66
  117.0 0.8 fusion.99
  117.9 6.3 %fusion.79 = bf16[1,512,64]{1,2,0:T(8,128)(2,1)S(1)} fusion(bf16[8192,64]{0,1:T(8,128)(2,1)} %param.41, bf16[512,8192]{1,0:T(8,128)(2,1)} %all-gather.2.cloned.1.call-done, f32[8192]{0:T(1024)S(1)} %copy-done.2, f32[512]{0:T(512)S(1)} %add_rsqrt_fusion), kind=kOutput, calls=%fused_computation.123 | convolution fusion | flops 553680896 | bytes 9537536 | tf_op jit(solution)/shard_map/dot_general | solution.py:67
  124.2 0.6 collective-permute-start.1
  124.8 0.8 subtract_convert_fusion
  126.7 7.3 %while.100 = (s32[]{:T(128)}, f32[2,256,4]{1,2,0:T(4,128)S(1)}, f32[2,256,4]{1,2,0:T(4,128)S(1)}, f32[2,256,4,128]{3,1,2,0:T(8,128)S(1)}, s32[]{:T(128)}, /*inde...) while((s32[]{:T(128)}, f32[2,256,4]{1,2,0:T(4,128)S(1)}, ...), condition=%wide.region_6.7_spmd.clone.clone, body=%wide.region_1.6_spmd.clone.clone.sunk | while | flops 273818368 | bytes 11925833 | solution.py:129
  126.8 0.6 dynamic_slice.54
  129.9 0.4 fusion.144
  130.4 0.6 dynamic_slice.54
  133.6 0.4 fusion.144
  134.0 109.9 %while.102 = (s32[]{:T(128)}, f32[2,256,4]{1,2,0:T(4,128)S(1)}, f32[2,256,4]{1,2,0:T(4,128)S(1)}, f32[2,256,4,128]{3,1,2,0:T(8,128)S(1)}, bf16[2,512,128]{2,1,0:...) while((s32[]{:T(128)}, f32[2,256,4]{1,2,0:T(4,128)S(1)}, ...), condition=%wide.region_14.15_spmd.clone.clone, body=%wide.region_7.14_spmd.clone.clone.sunk | while | flops 273818400 | bytes 13501441 | solution.py:145
  134.4 9.4 %collective-permute-done = bf16[2,512,128]{2,1,0:T(8,128)(2,1)S(1)} collective-permute-done((bf16[2,512,128]{2,1,0:T(8,128)(2,1)S(1)}, bf16[2,512,128]{2,1,0:T(8,128)(2,1)S(1)}, u32[]{:S(2)}, u32[]{:S(2)}) %collective-permute-start) | collective-permute-done | bytes 262176 | tf_op jit(solution)/shard_map/while/body/eval_jaxpr/ppermute | solution.py:30
  143.8 7.6 %while.103 = (s32[]{:T(128)}, f32[2,256,4]{1,2,0:T(4,128)S(1)}, f32[2,256,4]{1,2,0:T(4,128)S(1)}, f32[2,256,4,128]{3,1,2,0:T(8,128)S(1)}, s32[]{:T(128)}, /*inde...) while((s32[]{:T(128)}, f32[2,256,4]{1,2,0:T(4,128)S(1)}, ...), condition=%wide.region_13.13_spmd.clone, body=%wide.region_8.12_spmd.clone.sunk | while | flops 273818368 | bytes 11926865 | solution.py:129
  143.8 0.7 dynamic_slice.55
  147.2 0.4 fusion.157
  147.6 0.7 dynamic_slice.55
  151.0 0.4 fusion.157
  151.6 8.8 %collective-permute-done = bf16[2,512,128]{2,1,0:T(8,128)(2,1)S(1)} collective-permute-done((bf16[2,512,128]{2,1,0:T(8,128)(2,1)S(1)}, bf16[2,512,128]{2,1,0:T(8,128)(2,1)S(1)}, u32[]{:S(2)}, u32[]{:S(2)}) %collective-permute-start) | collective-permute-done | bytes 262176 | tf_op jit(solution)/shard_map/while/body/eval_jaxpr/ppermute | solution.py:30
  160.4 7.6 %while.103 = (s32[]{:T(128)}, f32[2,256,4]{1,2,0:T(4,128)S(1)}, f32[2,256,4]{1,2,0:T(4,128)S(1)}, f32[2,256,4,128]{3,1,2,0:T(8,128)S(1)}, s32[]{:T(128)}, /*inde...) while((s32[]{:T(128)}, f32[2,256,4]{1,2,0:T(4,128)S(1)}, ...), condition=%wide.region_13.13_spmd.clone, body=%wide.region_8.12_spmd.clone.sunk | while | flops 273818368 | bytes 11926865 | solution.py:129
  160.4 0.7 dynamic_slice.55
  163.7 0.4 fusion.157
  164.2 0.7 dynamic_slice.55
  167.5 0.4 fusion.157
  168.1 7.9 %collective-permute-done = bf16[2,512,128]{2,1,0:T(8,128)(2,1)S(1)} collective-permute-done((bf16[2,512,128]{2,1,0:T(8,128)(2,1)S(1)}, bf16[2,512,128]{2,1,0:T(8,128)(2,1)S(1)}, u32[]{:S(2)}, u32[]{:S(2)}) %collective-permute-start) | collective-permute-done | bytes 262176 | tf_op jit(solution)/shard_map/while/body/eval_jaxpr/ppermute | solution.py:30
  176.1 7.6 %while.103 = (s32[]{:T(128)}, f32[2,256,4]{1,2,0:T(4,128)S(1)}, f32[2,256,4]{1,2,0:T(4,128)S(1)}, f32[2,256,4,128]{3,1,2,0:T(8,128)S(1)}, s32[]{:T(128)}, /*inde...) while((s32[]{:T(128)}, f32[2,256,4]{1,2,0:T(4,128)S(1)}, ...), condition=%wide.region_13.13_spmd.clone, body=%wide.region_8.12_spmd.clone.sunk | while | flops 273818368 | bytes 11926865 | solution.py:129
  176.1 0.7 dynamic_slice.55
  179.4 0.4 fusion.157
  179.9 0.7 dynamic_slice.55
  183.2 0.4 fusion.157
  183.8 7.3 %collective-permute-done = bf16[2,512,128]{2,1,0:T(8,128)(2,1)S(1)} collective-permute-done((bf16[2,512,128]{2,1,0:T(8,128)(2,1)S(1)}, bf16[2,512,128]{2,1,0:T(8,128)(2,1)S(1)}, u32[]{:S(2)}, u32[]{:S(2)}) %collective-permute-start) | collective-permute-done | bytes 262176 | tf_op jit(solution)/shard_map/while/body/eval_jaxpr/ppermute | solution.py:30
  191.1 7.6 %while.103 = (s32[]{:T(128)}, f32[2,256,4]{1,2,0:T(4,128)S(1)}, f32[2,256,4]{1,2,0:T(4,128)S(1)}, f32[2,256,4,128]{3,1,2,0:T(8,128)S(1)}, s32[]{:T(128)}, /*inde...) while((s32[]{:T(128)}, f32[2,256,4]{1,2,0:T(4,128)S(1)}, ...), condition=%wide.region_13.13_spmd.clone, body=%wide.region_8.12_spmd.clone.sunk | while | flops 273818368 | bytes 11926865 | solution.py:129
  191.1 0.7 dynamic_slice.55
  194.5 0.4 fusion.157
  194.9 0.7 dynamic_slice.55
  198.3 0.4 fusion.157
  198.9 7.3 %collective-permute-done = bf16[2,512,128]{2,1,0:T(8,128)(2,1)S(1)} collective-permute-done((bf16[2,512,128]{2,1,0:T(8,128)(2,1)S(1)}, bf16[2,512,128]{2,1,0:T(8,128)(2,1)S(1)}, u32[]{:S(2)}, u32[]{:S(2)}) %collective-permute-start) | collective-permute-done | bytes 262176 | tf_op jit(solution)/shard_map/while/body/eval_jaxpr/ppermute | solution.py:30
  206.2 7.6 %while.103 = (s32[]{:T(128)}, f32[2,256,4]{1,2,0:T(4,128)S(1)}, f32[2,256,4]{1,2,0:T(4,128)S(1)}, f32[2,256,4,128]{3,1,2,0:T(8,128)S(1)}, s32[]{:T(128)}, /*inde...) while((s32[]{:T(128)}, f32[2,256,4]{1,2,0:T(4,128)S(1)}, ...), condition=%wide.region_13.13_spmd.clone, body=%wide.region_8.12_spmd.clone.sunk | while | flops 273818368 | bytes 11926865 | solution.py:129
  206.2 0.7 dynamic_slice.55
  209.5 0.4 fusion.157
  210.0 0.7 dynamic_slice.55
  213.3 0.4 fusion.157
  213.9 7.3 %collective-permute-done = bf16[2,512,128]{2,1,0:T(8,128)(2,1)S(1)} collective-permute-done((bf16[2,512,128]{2,1,0:T(8,128)(2,1)S(1)}, bf16[2,512,128]{2,1,0:T(8,128)(2,1)S(1)}, u32[]{:S(2)}, u32[]{:S(2)}) %collective-permute-start) | collective-permute-done | bytes 262176 | tf_op jit(solution)/shard_map/while/body/eval_jaxpr/ppermute | solution.py:30
  221.2 7.6 %while.103 = (s32[]{:T(128)}, f32[2,256,4]{1,2,0:T(4,128)S(1)}, f32[2,256,4]{1,2,0:T(4,128)S(1)}, f32[2,256,4,128]{3,1,2,0:T(8,128)S(1)}, s32[]{:T(128)}, /*inde...) while((s32[]{:T(128)}, f32[2,256,4]{1,2,0:T(4,128)S(1)}, ...), condition=%wide.region_13.13_spmd.clone, body=%wide.region_8.12_spmd.clone.sunk | while | flops 273818368 | bytes 11926865 | solution.py:129
  221.2 0.7 dynamic_slice.55
  224.5 0.4 fusion.157
  225.0 0.7 dynamic_slice.55
  228.4 0.4 fusion.157
  229.0 7.3 %collective-permute-done = bf16[2,512,128]{2,1,0:T(8,128)(2,1)S(1)} collective-permute-done((bf16[2,512,128]{2,1,0:T(8,128)(2,1)S(1)}, bf16[2,512,128]{2,1,0:T(8,128)(2,1)S(1)}, u32[]{:S(2)}, u32[]{:S(2)}) %collective-permute-start) | collective-permute-done | bytes 262176 | tf_op jit(solution)/shard_map/while/body/eval_jaxpr/ppermute | solution.py:30
  236.3 7.6 %while.103 = (s32[]{:T(128)}, f32[2,256,4]{1,2,0:T(4,128)S(1)}, f32[2,256,4]{1,2,0:T(4,128)S(1)}, f32[2,256,4,128]{3,1,2,0:T(8,128)S(1)}, s32[]{:T(128)}, /*inde...) while((s32[]{:T(128)}, f32[2,256,4]{1,2,0:T(4,128)S(1)}, ...), condition=%wide.region_13.13_spmd.clone, body=%wide.region_8.12_spmd.clone.sunk | while | flops 273818368 | bytes 11926865 | solution.py:129
  236.3 0.7 dynamic_slice.55
  239.6 0.4 fusion.157
  240.1 0.7 dynamic_slice.55
  243.4 0.4 fusion.157
  244.7 10.1 %convolution_convert_fusion = bf16[512,8192]{1,0:T(8,128)(2,1)} fusion(bf16[512,8192]{1,0:T(8,128)(2,1)} %param.42, bf16[64,8,4,128]{3,2,1,0:T(4,128)(2,1)S(1)} %bitcast.230), kind=kOutput, calls=%fused_computation.121 | convolution fusion | flops 4299161600 | bytes 17301504 | tf_op jit(solution)/shard_map/dot_general | solution.py:153
  254.8 0.6 log_add_fusion
  255.4 103.6 %reduce-scatter.2.cloned.1.call-done = bf16[512,512]{1,0:T(8,128)(2,1)} async-done(((bf16[512,8192]{1,0:T(8,128)(2,1)}), bf16[512,512]{1,0:T(8,128)(2,1)}) %reduce-scatter.2.cloned.1.call-update) | async-done | bytes 524304 | tf_op jit(solution)/shard_map/reduce_scatter | solution.py:154
  (262 shorter events, 34.7 us)
Async XLA Ops:
  7.2 103.1 %copy-start = (bf16[8192,64]{0,1:T(8,128)(2,1)S(1)}, bf16[8192,64]{0,1:T(8,128)(2,1)}, u32[]{:S(2)}) copy-start(bf16[8192,64]{0,1:T(8,128)(2,1)} %param.40) | copy-start | bytes 3145732
  7.2 90.9 %copy-start.2 = (f32[8192]{0:T(1024)S(1)}, f32[8192]{0:T(1024)}, u32[]{:S(2)}) copy-start(f32[8192]{0:T(1024)} %param.38) | copy-start | bytes 98308
  7.2 85.8 %all-gather.2.cloned.1.call-start = ((), (), s32[]{:S(2)}) async-start(), calls=%async_computation.1 | async-start | bytes 8912896 | tf_op jit(solution)/shard_map/all_gather | solution.py:61
  7.9 351.1 %reduce-scatter.2.cloned.1.call-start = ((), (), s32[]{:S(2)}) async-start(), calls=%async_computation.2 | async-start | bytes 8912896 | tf_op jit(solution)/shard_map/reduce_scatter | solution.py:154
  117.9 8.9 %copy-start.1 = (s32[16]{0:T(128)S(1)}, s32[16]{0:T(128)}, u32[]{:S(2)}) copy-start(s32[16]{0:T(128)} %param.43) | copy-start | bytes 196
  124.2 2.1 collective-permute-start.1
  134.0 9.8 %collective-permute-start = (bf16[2,512,128]{2,1,0:T(8,128)(2,1)S(1)}, bf16[2,512,128]{2,1,0:T(8,128)(2,1)S(1)}, u32[]{:S(2)}, u32[]{:S(2)}) collective-permute-start(bf16[2,512,128]{2,1,0:T(8,128)(2,1)S(1)} %get-tuple-element.2122), channel_id=1, source_target_pairs={{112,0},{0,16},{16,32},{32,48},{48,64},{64,80},{80,96},{96,112},{1... | collective-permute-start | bytes 786440 | tf_op jit(solution)/shard_map/while/body/eval_jaxpr/ppermute | solution.py:30
  151.5 8.9 %collective-permute-start = (bf16[2,512,128]{2,1,0:T(8,128)(2,1)S(1)}, bf16[2,512,128]{2,1,0:T(8,128)(2,1)S(1)}, u32[]{:S(2)}, u32[]{:S(2)}) collective-permute-start(bf16[2,512,128]{2,1,0:T(8,128)(2,1)S(1)} %get-tuple-element.2122), channel_id=1, source_target_pairs={{112,0},{0,16},{16,32},{32,48},{48,64},{64,80},{80,96},{96,112},{1... | collective-permute-start | bytes 786440 | tf_op jit(solution)/shard_map/while/body/eval_jaxpr/ppermute | solution.py:30
  168.0 8.0 %collective-permute-start = (bf16[2,512,128]{2,1,0:T(8,128)(2,1)S(1)}, bf16[2,512,128]{2,1,0:T(8,128)(2,1)S(1)}, u32[]{:S(2)}, u32[]{:S(2)}) collective-permute-start(bf16[2,512,128]{2,1,0:T(8,128)(2,1)S(1)} %get-tuple-element.2122), channel_id=1, source_target_pairs={{112,0},{0,16},{16,32},{32,48},{48,64},{64,80},{80,96},{96,112},{1... | collective-permute-start | bytes 786440 | tf_op jit(solution)/shard_map/while/body/eval_jaxpr/ppermute | solution.py:30
  183.7 7.4 %collective-permute-start = (bf16[2,512,128]{2,1,0:T(8,128)(2,1)S(1)}, bf16[2,512,128]{2,1,0:T(8,128)(2,1)S(1)}, u32[]{:S(2)}, u32[]{:S(2)}) collective-permute-start(bf16[2,512,128]{2,1,0:T(8,128)(2,1)S(1)} %get-tuple-element.2122), channel_id=1, source_target_pairs={{112,0},{0,16},{16,32},{32,48},{48,64},{64,80},{80,96},{96,112},{1... | collective-permute-start | bytes 786440 | tf_op jit(solution)/shard_map/while/body/eval_jaxpr/ppermute | solution.py:30
  198.8 7.4 %collective-permute-start = (bf16[2,512,128]{2,1,0:T(8,128)(2,1)S(1)}, bf16[2,512,128]{2,1,0:T(8,128)(2,1)S(1)}, u32[]{:S(2)}, u32[]{:S(2)}) collective-permute-start(bf16[2,512,128]{2,1,0:T(8,128)(2,1)S(1)} %get-tuple-element.2122), channel_id=1, source_target_pairs={{112,0},{0,16},{16,32},{32,48},{48,64},{64,80},{80,96},{96,112},{1... | collective-permute-start | bytes 786440 | tf_op jit(solution)/shard_map/while/body/eval_jaxpr/ppermute | solution.py:30
  213.8 7.4 %collective-permute-start = (bf16[2,512,128]{2,1,0:T(8,128)(2,1)S(1)}, bf16[2,512,128]{2,1,0:T(8,128)(2,1)S(1)}, u32[]{:S(2)}, u32[]{:S(2)}) collective-permute-start(bf16[2,512,128]{2,1,0:T(8,128)(2,1)S(1)} %get-tuple-element.2122), channel_id=1, source_target_pairs={{112,0},{0,16},{16,32},{32,48},{48,64},{64,80},{80,96},{96,112},{1... | collective-permute-start | bytes 786440 | tf_op jit(solution)/shard_map/while/body/eval_jaxpr/ppermute | solution.py:30
  228.9 7.4 %collective-permute-start = (bf16[2,512,128]{2,1,0:T(8,128)(2,1)S(1)}, bf16[2,512,128]{2,1,0:T(8,128)(2,1)S(1)}, u32[]{:S(2)}, u32[]{:S(2)}) collective-permute-start(bf16[2,512,128]{2,1,0:T(8,128)(2,1)S(1)} %get-tuple-element.2122), channel_id=1, source_target_pairs={{112,0},{0,16},{16,32},{32,48},{48,64},{64,80},{80,96},{96,112},{1... | collective-permute-start | bytes 786440 | tf_op jit(solution)/shard_map/while/body/eval_jaxpr/ppermute | solution.py:30
Sparse Core Ops, SparseCore 0:
  10.3 82.6 all-gather.1
  254.9 104.0 reduce-scatter.1
where the time goes:
time: 367 us; the launch traced here: 366 us
  waiting for transfers between devices  241 us (66%)
  matrix products  58.4 us (16%)
  other arithmetic  22.2 us (6%)
  between operations  15.6 us (4%)
  local copies, waits for them, and re-layouts  14.5 us (4%)
  loops' own time  12.6 us (3%)
    reduce_scatter x1, waiting for transfers between devices, shards(): lax.psum_scatter(partial_terms.astype(jnp.bfloat16), 'tp', scatter_dimens...  104 us
    all_gather x1, waiting for transfers between devices, shards(): gathered = lax.all_gather(checkpoint, 'tp', axis=1, tiled=True)  81.6 us
    ppermute x7, waiting for transfers between devices, from_behind(): return lax.ppermute(block, axis, route)  55.2 us
    dot_general x32, matrix products, absorb(): jnp.einsum('qhk,kd->qhd', weights.astype(jnp.bfloat16), value_rows, prefe...  13.8 us
    another operation x8, loops' own time, visit_rows(): return lax.fori_loop(0, block_count, one_block, running)  12.1 us
    dot_general x1, matrix products, shards(): jnp.dot(normed, query_weight, preferred_element_type=jnp.float32)  11.6 us
    dot_general x32, matrix products, absorb(): jnp.einsum('qhd,kd->qhk', query_rows, key_rows, preferred_element_type=jn...  10.5 us
    dynamic_slice x16, local copies, waits for them, and re-layouts, one_block(): key_block = lax.dynamic_index_in_dim(block_order, stored, 0, keepdims=False)  10.3 us
  transfers between devices with their start and end apart: 10, of which 9 were waited for; matrix products, arithmetic and copies ran while one was open for 1% of the time, Pallas kernels for 0%

commit v1 on v0

v1 whole, which is shorter than its diff:
```python
import functools
import math

import jax
import jax.numpy as jnp
from jax import lax
from jax.experimental import pallas as pl
from jax.experimental.pallas import tpu as pltpu
from jax.sharding import PartitionSpec as P

MESH = pl.DeviceIdType.MESH
HEAD = 128
ROWS = 256
FEAT = 512
HALF = ROWS // 2
N_TP = 16
N_CP = 8
D = 8192
rope_base = 500000.0
norm_epsilon = 1e-05
masked_score = -1e30
LN2 = math.log(2.0)

f32 = jnp.float32
bf16 = jnp.bfloat16


def pick(i, values):
    out = values[-1]
    for n in range(len(values) - 2, -1, -1):
        out = jnp.where(i == n, values[n], out)
    return out


class Gather:
    def __init__(self, slot, ssem, rsem, right, left, pair, core):
        self.slot, self.ssem, self.rsem = slot, ssem, rsem
        self.right, self.left, self.pair, self.core = right, left, pair, core
        self.blocks = [(0, 0), (3, 0), (1, 0), (2, 0), (0, 1), (3, 1), (1, 1), (2, 1)]

    def ref(self, c, dr, dp, dk=0, rows=None):
        ref = self.slot(c, dr, dp, dk)
        return ref if rows is None else ref.at[pl.ds(rows * HALF, HALF)]

    def copy(self, c, n, ref, device):
        return pltpu.make_async_remote_copy(
            src_ref=ref,
            dst_ref=ref,
            send_sem=self.ssem.at[c * 17 + n],
            recv_sem=self.rsem.at[c * 17 + n],
            device_id=device,
            device_id_type=MESH,
        )

    def send_core(self, c, b):
        self.copy(c, 9 + b, self.ref(c, *self.blocks[b]), self.core).start()

    def start(self, c):
        own = self.ref(c, 0, 0)
        self.copy(c, 8, own, self.pair).start()
        self.copy(c, 0, own, self.right).start()
        self.copy(c, 4, own, self.left).start()
        self.send_core(c, 0)

    def from_left(self, c, dp):
        self.copy(c, 2 * dp, self.ref(c, 3, dp), self.left).wait_recv()
        self.copy(c, 1 + 2 * dp, self.ref(c, 3, dp, rows=0), self.right).start()
        self.send_core(c, 1 + 4 * dp)

    def from_right(self, c, dp):
        self.copy(c, 4 + 2 * dp, self.ref(c, 1, dp), self.right).wait_recv()
        self.copy(c, 5 + 2 * dp, self.ref(c, 1, dp, rows=1), self.left).start()
        self.send_core(c, 2 + 4 * dp)

    def from_pair(self, c):
        block = self.ref(c, 0, 1)
        self.copy(c, 8, block, self.pair).wait_recv()
        self.copy(c, 2, block, self.right).start()
        self.copy(c, 6, block, self.left).start()
        self.send_core(c, 4)

    def from_far(self, c, dp):
        self.copy(c, 1 + 2 * dp, self.ref(c, 2, dp, rows=0), self.left).wait_recv()
        self.copy(c, 5 + 2 * dp, self.ref(c, 2, dp, rows=1), self.right).wait_recv()
        self.send_core(c, 3 + 4 * dp)

    def from_core(self, c, b):
        self.copy(c, 9 + b, self.ref(c, *self.blocks[b], dk=1), self.core).wait_recv()

    def drain(self, c):
        for n in range(17):
            half = n in (1, 3, 5, 7)
            ref = self.ref(c, 0, 0, rows=0 if half else None)
            self.copy(c, n, ref, self.core).wait_send()


def kernel(
    order, x_hbm, gain, cq, sq, ck, sk, wq_hbm, wkv_hbm, wo_hbm,
    proj, norm_out,
    xg, wq, wkv, wo, acc, ss, q, kvg, kt, v1, scr, top, outs, att, bias,
    ro, ra, rb, rc, rd, ry,
    x_sem, w_sem, wo_sem, gs, gr, ks, kr, rs, rr,
):
    tp, cp = lax.axis_index("tp"), lax.axis_index("cp")
    core, yh, xx = tp % 2, (tp // 2) % 2, tp // 4
    yl, zz = cp % 2, cp // 2

    def tpi(dr, dp, dk):
        return (((xx + dr) % 4) * 2 + (yh + dp) % 2) * 2 + (core + dk) % 2

    def cpi(dr, dp):
        return ((zz + dr) % 4) * 2 + (yl + dp) % 2

    right, left = {"tp": tpi(1, 0, 0)}, {"tp": tpi(3, 0, 0)}
    pair, other = {"tp": tpi(0, 1, 0)}, {"tp": tpi(0, 0, 1)}
    up, down, beside = {"cp": cpi(1, 0)}, {"cp": cpi(3, 0)}, {"cp": cpi(0, 1)}

    dr_of = (0, 0, 3, 1, 3, 1, 2, 2)
    dk_of = (0, 1, 0, 0, 1, 1, 0, 1)

    def slot_at(i):
        return tpi(pick(i % 8, dr_of), i // 8, pick(i % 8, dk_of))

    x_copies = [
        pltpu.make_async_copy(x_hbm.at[pl.ds(c * ROWS, ROWS)], xg.at[c, tp], x_sem.at[c])
        for c in range(2)
    ]
    for copy in x_copies:
        copy.start()

    def w_copies(i):
        rows = pl.ds(pl.multiple_of(slot_at(i) * FEAT, FEAT), FEAT)
        return (
            pltpu.make_async_copy(wq_hbm.at[rows], wq.at[rows], w_sem.at[i]),
            pltpu.make_async_copy(wkv_hbm.at[rows], wkv.at[rows], w_sem.at[16 + i]),
        )

    for i in range(16):
        for copy in w_copies(i):
            copy.start()
    wo_copy = pltpu.make_async_copy(wo_hbm, wo, wo_sem)
    wo_copy.start()

    barrier = pltpu.get_barrier_semaphore()
    neighbours = (right, left, pair, other, up, down, beside)
    for device in neighbours:
        pl.semaphore_signal(barrier, inc=1, device_id=device, device_id_type=MESH)
    pl.semaphore_wait(barrier, len(neighbours))

    g = Gather(lambda c, dr, dp, dk: xg.at[c, tpi(dr, dp, dk)], gs, gr, right, left, pair, other)
    kv = Gather(
        lambda c, dr, dp, dk: kvg.at[c, (core + dk) % 2, cpi(dr, dp)], ks, kr, up, down, beside, other
    )

    for c in range(2):
        x_copies[c].wait()
        g.start(c)

    row_id = lax.broadcasted_iota(jnp.int32, (ROWS, ROWS), 0)
    col_id = lax.broadcasted_iota(jnp.int32, (ROWS, ROWS), 1)
    bias[0] = jnp.zeros((ROWS, ROWS), f32)
    bias[1] = jnp.where(col_id <= row_id, 0.0, masked_score).astype(f32)
    bias[2] = jnp.full((ROWS, ROWS), masked_score, f32)
    acc[...] = jnp.zeros_like(acc)
    ss[...] = jnp.zeros_like(ss)

    def project(c, i):
        j = slot_at(i)
        wide = xg[c, j].astype(f32)
        square = wide * wide
        ss[c] += square[:, :128] + square[:, 128:256] + square[:, 256:384] + square[:, 384:]
        scaled = (wide * gain[pl.ds(j, 1), :]).astype(bf16)
        rows = pl.ds(pl.multiple_of(j * FEAT, FEAT), FEAT)
        acc[c, :, :FEAT] += jnp.dot(scaled, wq[rows, :], preferred_element_type=f32)
        acc[c, :, FEAT:] += jnp.dot(scaled, wkv[rows, :], preferred_element_type=f32)

    even = (lax.broadcasted_iota(jnp.int32, (ROWS, HEAD), 1) % 2) == 0

    def turn(y, cosine, sine):
        swapped = jnp.where(even, pltpu.roll(y, HEAD - 1, 1), pltpu.roll(y, 1, 1))
        return y * cosine + swapped * sine

    def finish(c):
        scale = lax.rsqrt(jnp.sum(ss[c], axis=1, keepdims=True) * (1.0 / D) + norm_epsilon)
        scale = jnp.broadcast_to(scale, (ROWS, HEAD))
        part = slice(c * ROWS, (c + 1) * ROWS)
        kvg[c, core, cp] = turn(acc[c, :, FEAT:] * scale, ck[part], sk[part]).astype(bf16)
        kv.start(c)
        for h in range(4):
            y = acc[c, :, h * HEAD : (h + 1) * HEAD] * scale
            q[c, h] = turn(y, cq[part], sq[part]).astype(bf16)

    def assemble(c, s):
        lower, upper = kvg[c, 0, s].astype(f32), kvg[c, 1, s].astype(f32)
        low = lax.broadcasted_iota(jnp.int32, (ROWS, HEAD), 1) < 64
        keys = jnp.where(low, lower, pltpu.roll(upper, 64, 1))
        values = jnp.where(low, pltpu.roll(lower, 64, 1), upper)
        kt[c, s] = keys.T.astype(bf16)
        v1[c, s, :, :HEAD] = values.astype(bf16)
        v1[c, s, :, HEAD:] = jnp.ones((ROWS, HEAD), bf16)

    def attend(qc, kc, h, first, last):
        query = q[qc, h]
        q_block = order[2 * cp + qc]
        best = None
        for s in range(N_CP):
            k_block = order[2 * s + kc]
            which = jnp.where(k_block < q_block, 0, jnp.where(k_block == q_block, 1, 2))
            scores = jnp.dot(query, kt[kc, s], preferred_element_type=f32) + bias[which]
            scr[:, s * ROWS : (s + 1) * ROWS] = scores
            here = jnp.maximum(scores[:, :HEAD], scores[:, HEAD:])
            best = here if best is None else jnp.maximum(best, here)
        new_top = jnp.broadcast_to(jnp.max(best, axis=1, keepdims=True), (ROWS, HEAD))
        if not first:
            old_top = top[qc, h]
            new_top = jnp.maximum(old_top, new_top)
        both = jnp.concatenate([new_top, new_top], axis=1)
        total = None
        for s in range(N_CP):
            weights = jnp.exp2(scr[:, s * ROWS : (s + 1) * ROWS] - both).astype(bf16)
            here = jnp.dot(weights, v1[kc, s], preferred_element_type=f32)
            total = here if total is None else total + here
        if not first:
            shrink = jnp.exp2(old_top - new_top)
            total = total + outs[qc, h] * jnp.concatenate([shrink, shrink], axis=1)
        if last:
            sums = total[:, HEAD:]
            columns = pl.ds(pl.multiple_of(h * HEAD, HEAD), HEAD)
            att[qc, :, columns] = (total[:, :HEAD] / sums).astype(bf16)
            normalizer = (new_top + jnp.log2(sums)) * LN2
            norm_out[pl.ds(h, 1), qc * ROWS : (qc + 1) * ROWS] = normalizer.T[:1]
        else:
            top[qc, h] = new_top
            outs[qc, h] = total

    def rs_copy(c, n, src, dst, device):
        return pltpu.make_async_remote_copy(
            src_ref=src,
            dst_ref=dst,
            send_sem=rs.at[c * 17 + n],
            recv_sem=rr.at[c * 17 + n],
            device_id=device,
            device_id_type=MESH,
        )

    def out_products(c):
        def one(i, unused):
            dp = 1 - i // 4
            dr = pick(i % 4, (2, 1, 3, 0))
            for dk, slot in ((1, i), (0, 8 + i)):
                columns = pl.ds(pl.multiple_of(tpi(dr, dp, dk) * FEAT, FEAT), FEAT)
                xg[c, slot] = jnp.dot(
                    att[c], wo[:, columns], preferred_element_type=f32
                ).astype(bf16)
                if dk == 1:
                    rs_copy(c, i, xg.at[c, i], ro.at[c, i], other).start()
            return unused

        lax.fori_loop(0, 8, one, 0)

    def both_cores(c, i):
        rs_copy(c, i, xg.at[c, i], ro.at[c, i], other).wait_recv()
        return xg[c, 8 + i].astype(f32) + ro[c, i].astype(f32)

    lo, hi = pl.ds(0, HALF), pl.ds(HALF, HALF)

    def far_out(c, p):
        i = 4 * p
        block = xg.at[c, 8 + i]
        block[...] = both_cores(c, i).astype(bf16)
        rs_copy(c, 8 + 4 * p, block.at[lo], ra.at[c, p], right).start()
        rs_copy(c, 9 + 4 * p, block.at[hi], rb.at[c, p], left).start()

    def near_out(c, p, side):
        i = 4 * p + 1 + side
        block = xg.at[c, 8 + i]
        term = both_cores(c, i)
        landed = (ra, rb)[side].at[c, p]
        rs_copy(c, 8 + side + 4 * p, landed, landed, left).wait_recv()
        moved = landed[...].astype(f32)
        if side == 0:
            block[:HALF] = (term[:HALF] + moved).astype(bf16)
            block[HALF:] = term[HALF:].astype(bf16)
        else:
            block[:HALF] = term[:HALF].astype(bf16)
            block[HALF:] = (term[HALF:] + moved).astype(bf16)
        rs_copy(
            c, 10 + side + 4 * p, block, (rc, rd)[side].at[c, p], (right, left)[side]
        ).start()

    def here_in(c, p):
        i = 4 * p + 3
        term = both_cores(c, i)
        for side in range(2):
            landed = (rc, rd)[side].at[c, p]
            rs_copy(c, 10 + side + 4 * p, landed, landed, left).wait_recv()
            term = term + landed[...].astype(f32)
        block = xg.at[c, 8 + i]
        if p == 0:
            block[...] = term.astype(bf16)
            rs_copy(c, 16, block, ry.at[c], pair).start()
        else:
            rs_copy(c, 16, block, ry.at[c], pair).wait_recv()
            proj[c * ROWS : (c + 1) * ROWS] = (term + ry[c].astype(f32)).astype(bf16)

    def rs_drain(c):
        whole, half = xg.at[c, 0], xg.at[c, 0, lo]
        for n in range(17):
            ref = half if n in (8, 9, 12, 13) else whole
            rs_copy(c, n, ref, ref, other).wait_send()

    def when(i, n, action):
        pl.when(i == n)(action)

    def gather_step(c, i):
        block_of = (None, 0, None, None, 1, 2, None, 3, None, 4, None, None, 5, 6, None, 7)
        if c == 0:
            for copy in w_copies(i):
                copy.wait()

        def events(n):
            if n == 2:
                g.from_left(c, 0) if c == 0 else None
            if n == 3:
                g.from_right(c, 0) if c == 0 else None
            if n == 6:
                if c == 0:
                    g.from_pair(0)
                    g.from_left(1, 0)
                    g.from_right(1, 0)
                g.from_far(c, 0)
            if n == 8 and c == 1:
                g.from_pair(1)
            if n == 10:
                g.from_left(c, 1)
            if n == 11:
                g.from_right(c, 1)
            if n == 14:
                g.from_far(c, 1)
            if block_of[n] is not None:
                g.from_core(c, block_of[n])
            if c == 1:
                if n == 1:
                    kv.from_left(0, 0)
                    kv.from_right(0, 0)
                if n == 3:
                    kv.from_pair(0)
                if n == 5:
                    kv.from_far(0, 0)
                    kv.from_left(0, 1)
                    kv.from_right(0, 1)
                if n == 7:
                    kv.from_far(0, 1)

        for n in range(1, 16):
            when(i, n, functools.partial(events, n))
        project(c, i)

    def steps(c):
        def one(i, unused):
            gather_step(c, i)
            return unused

        lax.fori_loop(0, 16, one, 0)

    def each(count, body):
        def one(i, unused):
            body(i)
            return unused

        lax.fori_loop(0, count, one, 0)

    def kv_landed(c):
        for b in range(8):
            kv.from_core(c, b)
        each(N_CP, functools.partial(assemble, c))

    steps(0)
    finish(0)
    steps(1)
    finish(1)
    kv_landed(0)
    g.drain(0)
    g.drain(1)

    each(4, lambda h: attend(0, 0, h, True, False))
    kv.from_left(1, 0)
    kv.from_right(1, 0)
    kv.from_pair(1)
    each(4, lambda h: attend(1, 0, h, True, False))
    kv.from_far(1, 0)
    kv.from_left(1, 1)
    kv.from_right(1, 1)
    kv.from_far(1, 1)
    kv_landed(1)
    each(4, lambda h: attend(0, 1, h, False, True))
    wo_copy.wait()
    out_products(0)
    far_out(0, 0)
    far_out(0, 1)

    def last_unit(h):
        attend(1, 1, h, False, True)

        def send(p):
            near_out(0, p, 0)
            near_out(0, p, 1)

        when(h, 1, lambda: send(0))
        when(h, 3, lambda: send(1))

    each(4, last_unit)
    out_products(1)
    far_out(1, 0)
    far_out(1, 1)
    here_in(0, 0)
    for p in range(2):
        near_out(1, p, 0)
        near_out(1, p, 1)
    here_in(0, 1)
    here_in(1, 0)
    here_in(1, 1)
    for c in range(2):
        kv.drain(c)
        rs_drain(c)


def shards(
    checkpoint, norm_gain, query_weight, key_weight, value_weight, output_weight, block_order
):
    context_rank, tensor_rank = lax.axis_index("cp"), lax.axis_index("tp")
    own_blocks = lax.dynamic_slice_in_dim(block_order, 2 * context_rank, 2)
    offsets = jnp.arange(ROWS, dtype=jnp.int32)
    positions = (own_blocks[:, None] * ROWS + offsets[None, :]).reshape(2 * ROWS).astype(f32)
    lane = jnp.arange(HEAD, dtype=jnp.int32)
    sign = jnp.where(lane % 2 == 0, -1.0, 1.0).astype(f32)
    scale = math.log2(math.e) / math.sqrt(HEAD)

    def table(first_pair):
        pairs = (first_pair + lane // 2).astype(f32)
        angles = positions[:, None] * (rope_base ** (-2.0 * pairs / HEAD))[None, :]
        return jnp.cos(angles), jnp.sin(angles) * sign

    cosine, sine = table(0)
    k_cosine, k_sine = table((tensor_rank % 2) * 32)
    is_key = (lane < 64)[None, :]
    k_cosine, k_sine = jnp.where(is_key, k_cosine, 1.0), jnp.where(is_key, k_sine, 0.0)
    kv_weight = jnp.concatenate([key_weight, value_weight], axis=1)

    vmem = pl.BlockSpec(memory_space=pltpu.VMEM)
    hbm = pl.BlockSpec(memory_space=pl.ANY)
    dma = pltpu.SemaphoreType.DMA
    return pl.pallas_call(
        kernel,
        out_shape=(
            jax.ShapeDtypeStruct((2 * ROWS, FEAT), bf16),
            jax.ShapeDtypeStruct((4, 2 * ROWS), f32),
        ),
        in_specs=[pl.BlockSpec(memory_space=pltpu.SMEM), hbm, vmem, vmem, vmem, vmem, vmem, hbm, hbm, hbm],
        out_specs=(vmem, vmem),
        scratch_shapes=[
            pltpu.VMEM((2, N_TP, ROWS, FEAT), bf16),
            pltpu.VMEM((D, FEAT), bf16),
            pltpu.VMEM((D, HEAD), bf16),
            pltpu.VMEM((FEAT, D), bf16),
            pltpu.VMEM((2, ROWS, FEAT + HEAD), f32),
            pltpu.VMEM((2, ROWS, HEAD), f32),
            pltpu.VMEM((2, 4, ROWS, HEAD), bf16),
            pltpu.VMEM((2, 2, N_CP, ROWS, HEAD), bf16),
            pltpu.VMEM((2, N_CP, HEAD, ROWS), bf16),
            pltpu.VMEM((2, N_CP, ROWS, 2 * HEAD), bf16),
            pltpu.VMEM((ROWS, N_CP * ROWS), f32),
            pltpu.VMEM((2, 4, ROWS, HEAD), f32),
            pltpu.VMEM((2, 4, ROWS, 2 * HEAD), f32),
            pltpu.VMEM((2, ROWS, FEAT), bf16),
            pltpu.VMEM((3, ROWS, ROWS), f32),
            pltpu.VMEM((2, 8, ROWS, FEAT), bf16),
            pltpu.VMEM((2, 2, HALF, FEAT), bf16),
            pltpu.VMEM((2, 2, HALF, FEAT), bf16),
            pltpu.VMEM((2, 2, ROWS, FEAT), bf16),
            pltpu.VMEM((2, 2, ROWS, FEAT), bf16),
            pltpu.VMEM((2, ROWS, FEAT), bf16),
            dma((2,)),
            dma((32,)),
            dma,
            dma((34,)),
            dma((34,)),
            dma((34,)),
            dma((34,)),
            dma((34,)),
            dma((34,)),
        ],
        compiler_params=pltpu.CompilerParams(
            collective_id=0, has_side_effects=True, vmem_limit_bytes=67000000
        ),
        name="sublayer",
    )(
        block_order,
        checkpoint,
        norm_gain.reshape(N_TP, FEAT),
        cosine * scale,
        sine * scale,
        k_cosine,
        k_sine,
        query_weight,
        kv_weight,
        output_weight,
    )


def solution(mesh):
    return jax.shard_map(
        shards,
        mesh=mesh,
        in_specs=(
            P("cp", "tp"),
            P(),
            P(None, "tp"),
            P(None, "tp"),
            P(None, "tp"),
            P("tp", None),
            P(),
        ),
        out_specs=(P("cp", "tp"), P("tp", "cp")),
        check_vma=False,
    )
```

time: 367 us -> 153 us (0.42)
  waiting for transfers between devices: 241 us -> 0 us
  Pallas kernels: 0 us -> 136 us
  matrix products: 58.4 us -> 0 us
  between operations: 15.6 us -> 0.69 us
  other arithmetic: 22.2 us -> 7.94 us
  loops' own time: 12.6 us -> 0 us
  local copies, waits for them, and re-layouts: 14.5 us -> 7.59 us
    pallas_call x0 -> x1, Pallas kernels: none -> 136 us  [shards(): pl.pallas_call(kernel, out_shape=(jax.ShapeDtypeStruct((2 * ROWS, FEAT),...]
    reduce_scatter x1 -> x0, waiting for transfers between devices: 104 us -> none  [shards(): lax.psum_scatter(partial_terms.astype(jnp.bfloat16), 'tp', scatter_dimens...]
    all_gather x1 -> x0, waiting for transfers between devices: 81.6 us -> none  [shards(): gathered = lax.all_gather(checkpoint, 'tp', axis=1, tiled=True)]
    dot_general x68 -> x0, matrix products: 58.4 us -> none  [the longest x32 13.8 us: absorb(): jnp.einsum('qhk,kd->qhd', weights.astype(jnp.bfloat16), value_rows, prefe...]
    ppermute x8 -> x0, waiting for transfers between devices: 55.2 us -> none  [the longest x7 55.2 us: from_behind(): return lax.ppermute(block, axis, route)]
    another operation x9 -> x0, loops' own time: 12.6 us -> none  [the longest x8 12.1 us: visit_rows(): return lax.fori_loop(0, block_count, one_block, running)]
    reduce_sum x33 -> x0, other arithmetic: 11.8 us -> none  [the longest x32 6.67 us: absorb(): new_total = totals[query_slot] * shrink + jnp.sum(weights, axis=-1)]
    dynamic_slice x16 -> x0, local copies, waits for them, and re-layouts: 10.3 us -> none  [one_block(): key_block = lax.dynamic_index_in_dim(block_order, stored, 0, keepdims=False)]
  transfers between devices with their start and end apart: 10 -> 0, of which waited for: 9 -> 0; matrix products, arithmetic and copies ran while one was open for 1% -> 0% of each run, Pallas kernels for 0% -> 0%
where the time goes in v1:
time: 153 us; the launch traced here: 152 us
  Pallas kernels  136 us (89%)
  other arithmetic  7.94 us (5%)
  local copies, waits for them, and re-layouts  7.59 us (5%)
    pallas_call x1, Pallas kernels, shards(): pl.pallas_call(kernel, out_shape=(jax.ShapeDtypeStruct((2 * ROWS, FEAT),...  136 us
    unnamed x9, local copies, waits for them, and re-layouts  6.97 us
    concatenate x1, other arithmetic, shards(): kv_weight = jnp.concatenate([key_weight, value_weight], axis=1)  4.07 us

profile of v1, /device:TPU:1, one launch (start us, length us, event | category | flops | bytes accessed | tf_op | source)
XLA Modules:
  0.0 152.1 jit_solution(7543149232770123894)
XLA Ops:
  0.7 0.7 dynamic-slice_multiply_fusion
  1.4 0.1 convert_bitcast_fusion
  1.5 0.0 copy-start
  1.5 3.0 %fusion.5 = (f32[512,128]{1,0:T(8,128)}, f32[512,128]{1,0:T(8,128)}, f32[512,128]{1,0:T(8,128)}, f32[512,128]{1,0:T(8,128)}) fusion(f32[128]{0:T(128)S(1)} %get-tuple-element.7, f32[128]{0:T(128)S(1)} %get-tuple-element.6, f32[512]{0:T(512)S(1)} %bitcast.3, pred[128]{0:T(512)(128)(4,1)S(1)} %iota_compare_fusion, f32[128]{0:T(128)S(1)} %multiply_power_fusion.1), kind=kLoop, calls=%fused_computation.10 | loop fusion | flops 524288 | bytes 1052288 | tf_op jit(solution)/shard_map/jit(_where)/select_n | solution.py:447
  4.5 2.0 %copy.10 = bf16[8192,64]{1,0:T(8,128)(2,1)S(1)} copy(bf16[8192,64]{0,1:T(8,128)(2,1)} %param.11) | data formatting | bytes 2097152 | tf_op args[4]
  6.6 0.0 copy-done
  6.6 1.8 %copy.9 = bf16[8192,64]{1,0:T(8,128)(2,1)} copy(bf16[8192,64]{0,1:T(8,128)(2,1)S(1)} %copy-done) | data formatting | bytes 2097152 | tf_op args[3]
  8.3 0.0 copy-start.1
  8.4 4.1 %pad_maximum_fusion.wkv_hbm = bf16[8192,128]{1,0:T(8,128)(2,1)} fusion(bf16[8192,64]{1,0:T(8,128)(2,1)S(1)} %copy.10, bf16[8192,64]{1,0:T(8,128)(2,1)} %copy.9), kind=kLoop, calls=%fused_computation | loop fusion | flops 4194304 | bytes 4194304 | tf_op jit(solution)/shard_map/concatenate | solution.py:448
  12.4 0.0 copy-done.1
  12.4 0.6 reshape.61.gain
  13.0 135.9 %sublayer.1 = (bf16[512,512]{1,0:T(8,128)(2,1)}, f32[4,512]{1,0:T(4,128)}) custom-call(s32[16]{0:T(128)} %order.1, bf16[512,512]{1,0:T(8,128)(2,1)} %x_hbm.1, f32[16,512]{1,0:T(8,128)} %reshape.61.gain, f32[512,128]{1,0:T(8,128)} %get-tuple-element.5.cq, f32[512,128]{1,0:T(8,128)} %get-tuple-element.4.sq, f32[512,128]{1,0:T(8,128)} %get-tuple-element.3.ck, ...), custom_call_target="tpu_custom_call" | custom-call | tf_op jit(solution)/shard_map/sublayer/pallas_call | solution.py:453
  148.9 1.9 %copy.14 = bf16[512,512]{1,0:T(8,128)(2,1)} copy(bf16[512,512]{1,0:T(8,128)(2,1)} %get-tuple-element.10) | data formatting | bytes 1048576
  150.8 1.3 copy.15
  (4 shorter events, 0.0 us)
Async XLA Ops:
  1.5 5.1 %copy-start = (bf16[8192,64]{0,1:T(8,128)(2,1)S(1)}, bf16[8192,64]{0,1:T(8,128)(2,1)}, u32[]{:S(2)}) copy-start(bf16[8192,64]{0,1:T(8,128)(2,1)} %param.10) | copy-start | bytes 3145732
  8.3 4.1 %copy-start.1 = (f32[8192]{0:T(1024)S(1)}, f32[8192]{0:T(1024)}, u32[]{:S(2)}) copy-start(f32[8192]{0:T(1024)} %param.8) | copy-start | bytes 98308

commit v2 on v1

v2 whole, which is shorter than its diff:
```python
import functools
import math

import jax
import jax.numpy as jnp
from jax import lax
from jax.experimental import pallas as pl
from jax.experimental.pallas import tpu as pltpu
from jax.sharding import PartitionSpec as P

MESH = pl.DeviceIdType.MESH
HEAD = 128
ROWS = 256
FEAT = 512
HALF = ROWS // 2
N_TP = 16
N_CP = 8
D = 8192
rope_base = 500000.0
norm_epsilon = 1e-05
masked_score = -1e30
LN2 = math.log(2.0)

f32 = jnp.float32
bf16 = jnp.bfloat16


def pick(i, values):
    out = values[-1]
    for n in range(len(values) - 2, -1, -1):
        out = jnp.where(i == n, values[n], out)
    return out


class Gather:
    def __init__(self, slot, ssem, rsem, right, left, pair, core):
        self.slot, self.ssem, self.rsem = slot, ssem, rsem
        self.right, self.left, self.pair, self.core = right, left, pair, core

    def ref(self, c, b, dk=0, rows=None):
        ref = self.slot(c, b, dk)
        return ref if rows is None else ref.at[pl.ds(rows * HALF, HALF)]

    def copy(self, c, n, ref, device):
        return pltpu.make_async_remote_copy(
            src_ref=ref,
            dst_ref=ref,
            send_sem=self.ssem.at[c * 16 + n],
            recv_sem=self.rsem.at[c * 16 + n],
            device_id=device,
            device_id_type=MESH,
        )

    def send_core(self, c, b):
        self.copy(c, 8 + b, self.ref(c, b), self.core).start()

    def start(self, c):
        own = self.ref(c, 0)
        self.copy(c, 6, own, self.pair).start()
        self.copy(c, 0, own, self.right).start()
        self.copy(c, 3, own, self.left).start()
        self.send_core(c, 0)

    def from_left(self, c):
        self.copy(c, 0, self.ref(c, 1), self.left).wait_recv()
        self.copy(c, 1, self.ref(c, 1, rows=0), self.right).start()
        self.send_core(c, 1)

    def from_right(self, c):
        self.copy(c, 3, self.ref(c, 2), self.right).wait_recv()
        self.copy(c, 4, self.ref(c, 2, rows=1), self.left).start()
        self.send_core(c, 2)

    def from_pair(self, c):
        block = self.ref(c, 4)
        self.copy(c, 6, block, self.pair).wait_recv()
        self.copy(c, 2, block, self.right).start()
        self.copy(c, 5, block, self.left).start()
        self.send_core(c, 4)

    def from_far(self, c):
        self.copy(c, 1, self.ref(c, 3, rows=0), self.left).wait_recv()
        self.copy(c, 4, self.ref(c, 3, rows=1), self.right).wait_recv()
        self.copy(c, 7, self.ref(c, 3), self.pair).start()
        self.send_core(c, 3)

    def from_sides(self, c):
        self.copy(c, 2, self.ref(c, 5), self.left).wait_recv()
        self.send_core(c, 5)
        self.copy(c, 5, self.ref(c, 6), self.right).wait_recv()
        self.send_core(c, 6)

    def from_last(self, c):
        self.copy(c, 7, self.ref(c, 7), self.pair).wait_recv()
        self.send_core(c, 7)

    def from_core(self, c, b):
        self.copy(c, 8 + b, self.ref(c, b, dk=1), self.core).wait_recv()

    def drain(self, c):
        for n in range(16):
            ref = self.ref(c, 0, rows=0 if n in (1, 4) else None)
            self.copy(c, n, ref, self.core).wait_send()


def kernel(
    order, x_hbm, gain, wq_hbm, wk_hbm, wv_hbm, wo_hbm,
    proj, norm_out,
    xg, wq, wkv, wo, acc, ss, cos_t, sin_t, q, kvg, kt, v1, scr_a, scr_b, top, outs, att, bias,
    ro, ra, rb, rc, rd, re, ry,
    x_sem, w_sem, wo_sem, gs, gr, ks, kr, rs, rr,
):
    tp, cp = lax.axis_index("tp"), lax.axis_index("cp")
    core, yh, xx = tp % 2, (tp // 2) % 2, tp // 4
    yl, zz = cp % 2, cp // 2

    def tpi(dr, dp, dk):
        return (((xx + dr) % 4) * 2 + (yh + dp) % 2) * 2 + (core + dk) % 2

    def cpi(dr, dp):
        return ((zz + dr) % 4) * 2 + (yl + dp) % 2

    right, left = {"tp": tpi(1, 0, 0)}, {"tp": tpi(3, 0, 0)}
    pair, other = {"tp": tpi(0, 1, 0)}, {"tp": tpi(0, 0, 1)}
    up, down, beside = {"cp": cpi(1, 0)}, {"cp": cpi(3, 0)}, {"cp": cpi(0, 1)}

    ring_of = (0, 3, 1, 2)

    def tp_slot(b, dk):
        dr = ring_of[b % 4] if isinstance(b, int) else pick(b % 4, ring_of)
        return tpi(dr, b // 4, dk)

    x_copies = [
        pltpu.make_async_copy(x_hbm.at[pl.ds(c * ROWS, ROWS)], xg.at[c, tp], x_sem.at[c])
        for c in range(2)
    ]
    for copy in x_copies:
        copy.start()

    def wq_copy(b, dk):
        rows = pl.ds(pl.multiple_of(tp_slot(b, dk) * FEAT, FEAT), FEAT)
        return pltpu.make_async_copy(wq_hbm.at[rows], wq.at[rows], w_sem.at[b * 2 + dk])

    wk_copy = pltpu.make_async_copy(wk_hbm, wkv.at[pl.ds(0, 64)], w_sem.at[16])
    wv_copy = pltpu.make_async_copy(wv_hbm, wkv.at[pl.ds(64, 64)], w_sem.at[17])
    wo_copy = pltpu.make_async_copy(wo_hbm, wo, wo_sem)

    barrier = pltpu.get_barrier_semaphore()
    neighbours = (right, left, pair, other, up, down, beside)
    for device in neighbours:
        pl.semaphore_signal(barrier, inc=1, device_id=device, device_id_type=MESH)

    wk_copy.start()
    wv_copy.start()
    for b in (0, 1, 2, 4, 3, 5, 6, 7):
        for dk in range(2):
            wq_copy(b, dk).start()
    wo_copy.start()

    pl.semaphore_wait(barrier, len(neighbours))

    g = Gather(lambda c, b, dk: xg.at[c, tp_slot(b, dk)], gs, gr, right, left, pair, other)
    kv = Gather(
        lambda c, b, dk: kvg.at[c, (core + dk) % 2, cpi(ring_of[b % 4], b // 4)],
        ks, kr, up, down, beside, other,
    )

    for c in range(2):
        x_copies[c].wait()
        g.start(c)

    row_id = lax.broadcasted_iota(jnp.int32, (ROWS, ROWS), 0)
    col_id = lax.broadcasted_iota(jnp.int32, (ROWS, ROWS), 1)
    bias[0] = jnp.zeros((ROWS, ROWS), f32)
    bias[1] = jnp.where(col_id <= row_id, 0.0, masked_score).astype(f32)
    bias[2] = jnp.full((ROWS, ROWS), masked_score, f32)
    acc[...] = jnp.zeros_like(acc)
    ss[...] = jnp.zeros_like(ss)

    even = (lax.broadcasted_iota(jnp.int32, (ROWS, HEAD), 1) % 2) == 0
    low = lax.broadcasted_iota(jnp.int32, (ROWS, HEAD), 1) < 64

    def make_tables():
        lane8 = lax.broadcasted_iota(jnp.int32, (8, HEAD), 1)
        rate8 = jnp.exp2((lane8 // 2).astype(f32) * (-2.0 / HEAD * math.log2(rope_base)))
        rate = jnp.broadcast_to(rate8[:1], (ROWS, HEAD))
        angle = lax.broadcasted_iota(jnp.int32, (ROWS, HEAD), 0).astype(f32) * rate
        cos_r, sin_r = jnp.cos(angle), jnp.sin(angle)
        sign = jnp.where(even, -1.0, 1.0).astype(f32)
        for c in range(2):
            start = (order[2 * cp + c] * ROWS).astype(f32) * rate8
            cos_b, sin_b = jnp.cos(start)[:1], jnp.sin(start)[:1]
            cos_t[c] = cos_b * cos_r - sin_b * sin_r
            sin_t[c] = (sin_b * cos_r + cos_b * sin_r) * sign

    make_tables()

    def project(c, b, dk):
        j = tp_slot(b, dk)
        wide = xg[c, j].astype(f32)
        square = wide * wide
        ss[c] += square[:, :128] + square[:, 128:256] + square[:, 256:384] + square[:, 384:]
        scaled = jnp.concatenate(
            [
                (wide[:, n * HEAD : (n + 1) * HEAD] * gain[pl.ds(4 * j + n, 1), :]).astype(bf16)
                for n in range(4)
            ],
            axis=1,
        )
        rows = pl.ds(pl.multiple_of(j * FEAT, FEAT), FEAT)
        acc[c, :, :FEAT] += jnp.dot(scaled, wq[rows, :], preferred_element_type=f32)
        acc[c, :, FEAT:] += lax.dot_general(
            scaled, wkv[:, rows], (((1,), (1,)), ((), ())), preferred_element_type=f32
        )

    def turn(y, cosine, sine):
        swapped = jnp.where(even, pltpu.roll(y, HEAD - 1, 1), pltpu.roll(y, 1, 1))
        return y * cosine + swapped * sine

    def finish(c):
        scale = lax.rsqrt(jnp.sum(ss[c], axis=1, keepdims=True) * (1.0 / D) + norm_epsilon)
        scale = jnp.broadcast_to(scale, (ROWS, HEAD))
        cosine, sine = cos_t[c], sin_t[c]
        k_cos = jnp.where(core == 0, cosine, pltpu.roll(cosine, 64, 1))
        k_sin = jnp.where(core == 0, sine, pltpu.roll(sine, 64, 1))
        k_cos, k_sin = jnp.where(low, k_cos, 1.0), jnp.where(low, k_sin, 0.0)
        kvg[c, core, cp] = turn(acc[c, :, FEAT:] * scale, k_cos, k_sin).astype(bf16)
        kv.start(c)
        q_scale = scale * (math.log2(math.e) / math.sqrt(HEAD))
        for h in range(4):
            y = acc[c, :, h * HEAD : (h + 1) * HEAD] * q_scale
            q[c, h] = turn(y, cosine, sine).astype(bf16)

    def assemble(c, s):
        lower, upper = kvg[c, 0, s].astype(f32), kvg[c, 1, s].astype(f32)
        keys = jnp.where(low, lower, pltpu.roll(upper, 64, 1))
        values = jnp.where(low, pltpu.roll(lower, 64, 1), upper)
        kt[c, s] = keys.T.astype(bf16)
        rows = pl.ds(pl.multiple_of(s * ROWS, ROWS), ROWS)
        v1[c, rows, :HEAD] = values.astype(bf16)
        v1[c, rows, HEAD:] = jnp.ones((ROWS, HEAD), bf16)

    def unit(qc, kc, first, last, between=()):
        q_block = order[2 * cp + qc]
        which = []
        for s in range(N_CP):
            k_block = order[2 * s + kc]
            which.append(jnp.where(k_block < q_block, 0, jnp.where(k_block == q_block, 1, 2)))
        group = 4
        tops = {}

        def score(h, s, best):
            scr = (scr_a, scr_b)[h % 2]
            scores = jnp.dot(q[qc, h], kt[kc, s], preferred_element_type=f32) + bias[which[s]]
            scr[:, s * ROWS : (s + 1) * ROWS] = scores
            here = jnp.maximum(scores[:, :HEAD], scores[:, HEAD:])
            return here if best is None else jnp.maximum(best, here)

        def settle(h, best):
            new_top = jnp.broadcast_to(jnp.max(best, axis=1, keepdims=True), (ROWS, HEAD))
            tops[h] = new_top if first else jnp.maximum(top[qc, h], new_top)

        def weigh(h, s, total):
            scr = (scr_a, scr_b)[h % 2]
            both = jnp.concatenate([tops[h]] * 2, axis=1)
            weights = [
                jnp.exp2(scr[:, n * ROWS : (n + 1) * ROWS] - both).astype(bf16)
                for n in range(s, s + group)
            ]
            here = jnp.dot(
                jnp.concatenate(weights, axis=1),
                v1[kc, s * ROWS : (s + group) * ROWS],
                preferred_element_type=f32,
            )
            return here if total is None else total + here

        def close(h, total):
            if not first:
                shrink = jnp.exp2(top[qc, h] - tops[h])
                total = total + outs[qc, h] * jnp.concatenate([shrink, shrink], axis=1)
            if last:
                sums = total[:, HEAD:]
                att[qc, :, h * HEAD : (h + 1) * HEAD] = (total[:, :HEAD] / sums).astype(bf16)
                normalizer = (tops[h] + jnp.log2(sums)) * LN2
                norm_out[h : h + 1, qc * ROWS : (qc + 1) * ROWS] = normalizer.T[:1]
            else:
                top[qc, h] = tops[h]
                outs[qc, h] = total

        best = None
        for s in range(N_CP):
            best = score(0, s, best)
        settle(0, best)
        for h in range(4):
            best = total = None
            for s in range(N_CP):
                if h < 3:
                    best = score(h + 1, s, best)
                if s % group == group - 1:
                    total = weigh(h, s - group + 1, total)
            close(h, total)
            if h < 3:
                settle(h + 1, best)
            if h < len(between) and between[h] is not None:
                between[h]()

    def rs_copy(c, n, src, dst, device):
        return pltpu.make_async_remote_copy(
            src_ref=src,
            dst_ref=dst,
            send_sem=rs.at[c * 16 + n],
            recv_sem=rr.at[c * 16 + n],
            device_id=device,
            device_id_type=MESH,
        )

    lo, hi = pl.ds(0, HALF), pl.ds(HALF, HALF)
    dests = ((2, 1), (2, 0), (1, 1), (3, 1), (1, 0), (3, 0), (0, 1), (0, 0))

    def both_cores(c, i):
        rs_copy(c, i, xg.at[c, i], ro.at[c, i], other).wait_recv()
        return xg[c, 8 + i].astype(f32) + ro[c, i].astype(f32)

    def far_pair(c):
        block = xg.at[c, 8]
        block[...] = both_cores(c, 0).astype(bf16)
        rs_copy(c, 8, block, re.at[c], pair).start()

    def far_out(c):
        block = xg.at[c, 9]
        term = both_cores(c, 1)
        rs_copy(c, 8, re.at[c], re.at[c], pair).wait_recv()
        block[...] = (term + re[c].astype(f32)).astype(bf16)
        rs_copy(c, 9, block.at[lo], ra.at[c], right).start()
        rs_copy(c, 10, block.at[hi], rb.at[c], left).start()

    def near_pair(c, side):
        block = xg.at[c, 10 + side]
        block[...] = both_cores(c, 2 + side).astype(bf16)
        rs_copy(c, 11 + side, block, (rc, rd)[side].at[c, 1], (right, left)[side]).start()

    def near_out(c, side):
        block = xg.at[c, 12 + side]
        term = both_cores(c, 4 + side)
        landed = (ra, rb)[side].at[c]
        rs_copy(c, 9 + side, landed, landed, left).wait_recv()
        moved = landed[...].astype(f32)
        if side == 0:
            block[:HALF] = (term[:HALF] + moved).astype(bf16)
            block[HALF:] = term[HALF:].astype(bf16)
        else:
            block[:HALF] = term[:HALF].astype(bf16)
            block[HALF:] = (term[HALF:] + moved).astype(bf16)
        rs_copy(c, 13 + side, block, (rc, rd)[side].at[c, 0], (right, left)[side]).start()

    def here_in(c, p):
        term = both_cores(c, 7 - p)
        for side in range(2):
            landed = (rc, rd)[side].at[c, p]
            rs_copy(c, (13, 11)[p] + side, landed, landed, left).wait_recv()
            term = term + landed[...].astype(f32)
        block = xg.at[c, 14]
        if p == 1:
            block[...] = term.astype(bf16)
            rs_copy(c, 15, block, ry.at[c], pair).start()
        else:
            rs_copy(c, 15, block, ry.at[c], pair).wait_recv()
            proj[c * ROWS : (c + 1) * ROWS] = (term + ry[c].astype(f32)).astype(bf16)

    def rs_drain(c):
        whole, half = xg.at[c, 0], xg.at[c, 0, lo]
        for n in range(16):
            ref = half if n in (9, 10) else whole
            rs_copy(c, n, ref, ref, other).wait_send()

    def when(i, n, action):
        pl.when(i == n)(action)

    def out_products(c, events):
        def one(i, unused):
            dr, dp = pick(i, [d[0] for d in dests]), pick(i, [d[1] for d in dests])
            for dk, slot in ((1, i), (0, 8 + i)):
                columns = pl.ds(pl.multiple_of(tpi(dr, dp, dk) * FEAT, FEAT), FEAT)
                xg[c, slot] = jnp.dot(
                    att[c], wo[:, columns], preferred_element_type=f32
                ).astype(bf16)
                if dk == 1:
                    rs_copy(c, i, xg.at[c, i], ro.at[c, i], other).start()
            for n, action in events.items():
                when(i, n, action)
            return unused

        lax.fori_loop(0, 8, one, 0)

    plan = (
        [(c, 0, dk) for dk in range(2) for c in range(2)]
        + [(0, 1, 0), (0, 2, 0), (0, 1, 1), (0, 2, 1)]
        + [(1, 1, 0), (1, 2, 0), (1, 1, 1), (1, 2, 1)]
        + [(0, 4, 0), (0, 4, 1), (1, 4, 0), (1, 4, 1)]
        + [(0, 3, 0), (0, 3, 1), (1, 3, 0), (1, 3, 1)]
        + [(0, 5, 0), (0, 6, 0), (0, 5, 1), (0, 6, 1)]
        + [(0, 7, 0), (0, 7, 1), (1, 7, 0), (1, 7, 1)]
        + [(1, 5, 0), (1, 6, 0), (1, 5, 1), (1, 6, 1)]
    )

    def gather_event(n):
        if n == 4:
            g.from_left(0)
            g.from_right(0)
        if n == 8:
            g.from_left(1)
            g.from_right(1)
            g.from_pair(0)
            g.from_pair(1)
        if n in (16, 18):
            g.from_far((n - 16) // 2)
        if n == 20:
            g.from_sides(0)
        if n == 24:
            g.from_last(0)
        if n == 26:
            g.from_last(1)
        if n == 28:
            kv.from_left(0)
            kv.from_right(0)
            kv.from_pair(0)
            g.from_sides(1)
        c, b, dk = plan[n]
        if dk:
            g.from_core(c, b)

    def steps(first, last):
        def one(i, unused):
            for n in range(first, last):
                if n in (4, 8, 16, 18, 20, 24, 26, 28) or plan[n][2]:
                    when(i, n, functools.partial(gather_event, n))
            code = pick(i - first, [(c * 8 + b) * 2 + dk for c, b, dk in plan[first:last]])
            c, b, dk = code // 16, (code // 2) % 8, code % 2
            pl.when(c == 0)(lambda: wq_copy(b, dk).wait())
            project(c, b, dk)
            return unused

        lax.fori_loop(first, last, one, 0)

    def each(count, body):
        def one(i, unused):
            body(i)
            return unused

        lax.fori_loop(0, count, one, 0)

    def kv_landed(c):
        for b in range(8):
            kv.from_core(c, b)
        each(N_CP, functools.partial(assemble, c))

    wk_copy.wait()
    wv_copy.wait()
    steps(0, 26)
    finish(0)
    steps(26, 32)
    finish(1)
    kv.from_far(0)
    kv.from_sides(0)
    kv.from_last(0)
    kv_landed(0)
    g.drain(0)
    g.drain(1)

    def sides1():
        kv.from_left(1)
        kv.from_right(1)
        kv.from_pair(1)

    def rest1():
        kv.from_far(1)
        kv.from_sides(1)

    unit(0, 0, True, False, (None, sides1, None, lambda: kv.from_far(1)))
    unit(1, 0, True, False, (lambda: kv.from_sides(1), lambda: kv.from_last(1)))
    kv_landed(1)
    unit(0, 1, False, True)
    wo_copy.wait()

    def first_sends(c):
        return {
            1: lambda: far_pair(c),
            3: lambda: near_pair(c, 0),
            4: lambda: near_pair(c, 1),
        }

    out_products(0, first_sends(0))
    unit(1, 1, False, True, (None, None, lambda: far_out(0), None))
    out_products(1, first_sends(1))
    here_in(0, 1)
    near_out(0, 0)
    near_out(0, 1)
    far_out(1)
    here_in(1, 1)
    near_out(1, 0)
    near_out(1, 1)
    here_in(0, 0)
    here_in(1, 0)
    for c in range(2):
        kv.drain(c)
        rs_drain(c)

def shards(
    checkpoint, norm_gain, query_weight, key_weight, value_weight, output_weight, block_order
):
    vmem = pl.BlockSpec(memory_space=pltpu.VMEM)
    hbm = pl.BlockSpec(memory_space=pl.ANY)
    dma = pltpu.SemaphoreType.DMA
    return pl.pallas_call(
        kernel,
        out_shape=(
            jax.ShapeDtypeStruct((2 * ROWS, FEAT), bf16),
            jax.ShapeDtypeStruct((4, 2 * ROWS), f32),
        ),
        in_specs=[pl.BlockSpec(memory_space=pltpu.SMEM), hbm, vmem, hbm, hbm, hbm, hbm],
        out_specs=(vmem, vmem),
        scratch_shapes=[
            pltpu.VMEM((2, N_TP, ROWS, FEAT), bf16),
            pltpu.VMEM((D, FEAT), bf16),
            pltpu.VMEM((HEAD, D), bf16),
            pltpu.VMEM((FEAT, D), bf16),
            pltpu.VMEM((2, ROWS, FEAT + HEAD), f32),
            pltpu.VMEM((2, ROWS, HEAD), f32),
            pltpu.VMEM((2, ROWS, HEAD), f32),
            pltpu.VMEM((2, ROWS, HEAD), f32),
            pltpu.VMEM((2, 4, ROWS, HEAD), bf16),
            pltpu.VMEM((2, 2, N_CP, ROWS, HEAD), bf16),
            pltpu.VMEM((2, N_CP, HEAD, ROWS), bf16),
            pltpu.VMEM((2, N_CP * ROWS, 2 * HEAD), bf16),
            pltpu.VMEM((ROWS, N_CP * ROWS), f32),
            pltpu.VMEM((ROWS, N_CP * ROWS), f32),
            pltpu.VMEM((2, 4, ROWS, HEAD), f32),
            pltpu.VMEM((2, 4, ROWS, 2 * HEAD), f32),
            pltpu.VMEM((2, ROWS, FEAT), bf16),
            pltpu.VMEM((3, ROWS, ROWS), f32),
            pltpu.VMEM((2, 8, ROWS, FEAT), bf16),
            pltpu.VMEM((2, HALF, FEAT), bf16),
            pltpu.VMEM((2, HALF, FEAT), bf16),
            pltpu.VMEM((2, 2, ROWS, FEAT), bf16),
            pltpu.VMEM((2, 2, ROWS, FEAT), bf16),
            pltpu.VMEM((2, ROWS, FEAT), bf16),
            pltpu.VMEM((2, ROWS, FEAT), bf16),
            dma((2,)),
            dma((18,)),
            dma,
            dma((32,)),
            dma((32,)),
            dma((32,)),
            dma((32,)),
            dma((32,)),
            dma((32,)),
        ],
        compiler_params=pltpu.CompilerParams(
            collective_id=0, has_side_effects=True, vmem_limit_bytes=67000000
        ),
        name="sublayer",
    )(
        block_order,
        checkpoint,
        norm_gain.reshape(D // HEAD, HEAD),
        query_weight,
        key_weight.T,
        value_weight.T,
        output_weight,
    )


def solution(mesh):
    return jax.shard_map(
        shards,
        mesh=mesh,
        in_specs=(
            P("cp", "tp"),
            P(),
            P(None, "tp"),
            P(None, "tp"),
            P(None, "tp"),
            P("tp", None),
            P(),
        ),
        out_specs=(P("cp", "tp"), P("tp", "cp")),
        check_vma=False,
    )
```

time: 153 us -> 110 us (0.72)
  Pallas kernels: 136 us -> 105 us
  other arithmetic: 7.94 us -> 0 us
  local copies, waits for them, and re-layouts: 7.59 us -> 3.16 us
    pallas_call x1, Pallas kernels: 136 us -> 105 us  [shards(): pl.pallas_call(kernel, out_shape=(jax.ShapeDtypeStruct((2 * ROWS, FEAT),...]
    concatenate x1 -> x0, other arithmetic: 4.07 us -> none  [shards(): kv_weight = jnp.concatenate([key_weight, value_weight], axis=1)]
    unnamed x9 -> x2, local copies, waits for them, and re-layouts: 6.97 us -> 3.16 us
    select_n x2 -> x0, other arithmetic: 3.04 us -> none  [the longest x1 3.03 us: shards(): jnp.where(is_key, k_sine, 0.0)]
where the time goes in v2:
time: 110 us; the launch traced here: 109 us
  Pallas kernels  105 us (95%)
  local copies, waits for them, and re-layouts  3.16 us (3%)
    pallas_call x1, Pallas kernels, shards(): pl.pallas_call(kernel, out_shape=(jax.ShapeDtypeStruct((2 * ROWS, FEAT),...  105 us
    unnamed x2, local copies, waits for them, and re-layouts  3.16 us

profile of v2, /device:TPU:1, one launch (start us, length us, event | category | flops | bytes accessed | tf_op | source)
XLA Modules:
  0.0 109.1 jit_solution(17628338449627906062)
XLA Ops:
  0.6 105.3 %sublayer.1 = (bf16[512,512]{1,0:T(8,128)(2,1)}, f32[4,512]{1,0:T(4,128)}) custom-call(s32[16]{0:T(128)} %order.1, bf16[512,512]{1,0:T(8,128)(2,1)} %x_hbm.1, f32[64,128]{1,0:T(8,128)} %bitcast.5, bf16[8192,512]{1,0:T(8,128)(2,1)} %wq_hbm.1, bf16[64,8192]{1,0:T(8,128)(2,1)} %bitcast.3, bf16[64,8192]{1,0:T(8,128)(2,1)} %bitcast.4, bf16[512,8192]{1,0:T(8,128)(2,1)} %wo_hbm.1), custom_call_target="tpu_custom_call" | custom-call | tf_op jit(solution)/shard_map/sublayer/pallas_call | solution.py:514
  106.0 1.9 %copy.11 = bf16[512,512]{1,0:T(8,128)(2,1)} copy(bf16[512,512]{1,0:T(8,128)(2,1)} %get-tuple-element.4) | data formatting | bytes 1048576
  107.8 1.3 %copy.12 = f32[4,512]{1,0:T(4,128)} copy(f32[4,512]{1,0:T(4,128)} %get-tuple-element.5) | data formatting | bytes 16384

commit v3 on v2

v3 whole, which is shorter than its diff:
```python
import functools
import math

import jax
import jax.numpy as jnp
from jax import lax
from jax.experimental import pallas as pl
from jax.experimental.pallas import tpu as pltpu
from jax.sharding import PartitionSpec as P

MESH = pl.DeviceIdType.MESH
HEAD = 128
ROWS = 256
FEAT = 512
HALF = ROWS // 2
N_TP = 16
N_CP = 8
D = 8192
rope_base = 500000.0
norm_epsilon = 1e-05
masked_score = -1e30
LN2 = math.log(2.0)

f32 = jnp.float32
bf16 = jnp.bfloat16


def pick(i, values):
    out = values[-1]
    for n in range(len(values) - 2, -1, -1):
        out = jnp.where(i == n, values[n], out)
    return out


class Gather:
    def __init__(self, slot, ssem, rsem, right, left, pair, core=None):
        self.slot, self.ssem, self.rsem = slot, ssem, rsem
        self.right, self.left, self.pair, self.core = right, left, pair, core
        self.count = 10 if core is None else 18

    def ref(self, c, b, dk=0, rows=None):
        ref = self.slot(c, b, dk)
        return ref if rows is None else ref.at[pl.ds(rows * HALF, HALF)]

    def copy(self, c, n, ref, device):
        return pltpu.make_async_remote_copy(
            src_ref=ref,
            dst_ref=ref,
            send_sem=self.ssem.at[c * self.count + n],
            recv_sem=self.rsem.at[c * self.count + n],
            device_id=device,
            device_id_type=MESH,
        )

    def send_core(self, c, b):
        if self.core is not None:
            self.copy(c, 10 + b, self.ref(c, b), self.core).start()

    def start_pair(self, c):
        self.copy(c, 8, self.ref(c, 0), self.pair).start()
        self.send_core(c, 0)

    def start_ring(self, c):
        lower, upper = self.ref(c, 0, rows=0), self.ref(c, 0, rows=1)
        self.copy(c, 0, lower, self.right).start()
        self.copy(c, 4, upper, self.left).start()
        self.copy(c, 1, upper, self.right).start()
        self.copy(c, 5, lower, self.left).start()

    def pass_on(self, c):
        block = self.ref(c, 1, rows=0)
        self.copy(c, 0, block, self.left).wait_recv()
        self.copy(c, 2, block, self.right).start()
        block = self.ref(c, 2, rows=1)
        self.copy(c, 4, block, self.right).wait_recv()
        self.copy(c, 6, block, self.left).start()

    def from_sides(self, c):
        self.copy(c, 1, self.ref(c, 1, rows=1), self.left).wait_recv()
        self.send_core(c, 1)
        self.copy(c, 5, self.ref(c, 2, rows=0), self.right).wait_recv()
        self.send_core(c, 2)

    def from_pair(self, c):
        self.copy(c, 8, self.ref(c, 4), self.pair).wait_recv()
        self.send_core(c, 4)

    def pass_pair(self, c):
        block = self.ref(c, 4)
        self.copy(c, 3, block, self.right).start()
        self.copy(c, 7, block, self.left).start()

    def from_far(self, c):
        self.copy(c, 2, self.ref(c, 3, rows=0), self.left).wait_recv()
        self.copy(c, 6, self.ref(c, 3, rows=1), self.right).wait_recv()
        self.copy(c, 9, self.ref(c, 3), self.pair).start()
        self.send_core(c, 3)

    def from_pair_sides(self, c):
        self.copy(c, 3, self.ref(c, 5), self.left).wait_recv()
        self.send_core(c, 5)
        self.copy(c, 7, self.ref(c, 6), self.right).wait_recv()
        self.send_core(c, 6)

    def from_last(self, c):
        self.copy(c, 9, self.ref(c, 7), self.pair).wait_recv()
        self.send_core(c, 7)

    def from_core(self, c, b):
        self.copy(c, 10 + b, self.ref(c, b, dk=1), self.core).wait_recv()

    def drain(self, c):
        for n in range(self.count):
            ref = self.ref(c, 0, rows=0 if n in (0, 1, 2, 4, 5, 6) else None)
            self.copy(c, n, ref, self.pair).wait_send()


RING = (0, 3, 1, 2)
KEY_ORDER = (0, 1, 2, 4, 3, 5, 6, 7)
DESTS = ((2, 1), (2, 0), (1, 1), (3, 1), (1, 0), (3, 0), (0, 1), (0, 0))
PLAN = (
    (0, 0), (1, 0), (0, 1), (0, 2), (0, 4), (0, 3), (1, 1), (1, 2),
    (1, 4), (1, 3), (0, 7), (0, 5), (0, 6), (1, 7), (1, 5), (1, 6),
)


def kernel(
    order, x_hbm, gain, wq_hbm, wk_hbm, wv_hbm, wo_hbm,
    proj, norm_out,
    xg, wq, wkv, wo, acc_q, acc_kv, ss, part, part_q, part_kv, cos_t, sin_t, q, kvg, kt, v1,
    scr_a, scr_b, top, outs, att, bias, terms, ra, rb, rc, rd, re, ry,
    x_sem, w_sem, xs, xr, gs, gr, ks, kr, ps, pr, rs, rr,
):
    tp, cp = lax.axis_index("tp"), lax.axis_index("cp")
    core, yh, xx = tp % 2, (tp // 2) % 2, tp // 4
    yl, zz = cp % 2, cp // 2

    def tpi(dr, dp, dk):
        return (((xx + dr) % 4) * 2 + (yh + dp) % 2) * 2 + (core + dk) % 2

    def cpi(dr, dp):
        return ((zz + dr) % 4) * 2 + (yl + dp) % 2

    right, left = {"tp": tpi(1, 0, 0)}, {"tp": tpi(3, 0, 0)}
    pair, other = {"tp": tpi(0, 1, 0)}, {"tp": tpi(0, 0, 1)}
    up, down, beside = {"cp": cpi(1, 0)}, {"cp": cpi(3, 0)}, {"cp": cpi(0, 1)}

    def chip(b):
        dr = RING[b % 4] if isinstance(b, int) else pick(b % 4, RING)
        return ((xx + dr) % 4) * 2 + (yh + b // 4) % 2

    def tp_slot(b, dk):
        return chip(b) * 2 + (core + dk) % 2

    def kv_slot(b):
        dr = RING[b % 4] if isinstance(b, int) else pick(b % 4, RING)
        return cpi(dr, b // 4)

    x_copies = [
        pltpu.make_async_copy(x_hbm.at[pl.ds(c * ROWS, ROWS)], xg.at[c, tp // 2], x_sem.at[c])
        for c in range(2)
    ]
    for copy in x_copies:
        copy.start()

    def features(b, dk):
        return pl.ds(pl.multiple_of(tp_slot(b, dk) * FEAT, FEAT), FEAT)

    def to_other(n, src, dst):
        return pltpu.make_async_remote_copy(
            src_ref=src,
            dst_ref=dst,
            send_sem=xs.at[n],
            recv_sem=xr.at[n],
            device_id=other,
            device_id_type=MESH,
        )

    def wq_copy(b):
        return pltpu.make_async_copy(wq_hbm.at[features(b, 0)], wq.at[0, b], w_sem.at[b])

    def wo_copy(b):
        return pltpu.make_async_copy(wo_hbm.at[:, features(b, 0)], wo.at[0, b], w_sem.at[8 + b])

    def wq_across(b):
        return to_other(b, wq_hbm.at[features(b, 1)], wq.at[1, b])

    def wo_across(b):
        return to_other(8 + b, wo_hbm.at[:, features(b, 1)], wo.at[1, b])

    wk_copy = pltpu.make_async_copy(wk_hbm, wkv.at[pl.ds(0, 64)], w_sem.at[16])
    wv_copy = pltpu.make_async_copy(wv_hbm, wkv.at[pl.ds(64, 64)], w_sem.at[17])
    wk_across = to_other(16, wk_hbm, wkv.at[pl.ds(128, 64)])
    wv_across = to_other(17, wv_hbm, wkv.at[pl.ds(192, 64)])

    barrier = pltpu.get_barrier_semaphore()
    neighbours = (right, left, pair, other, up, down, beside)
    for device in neighbours:
        pl.semaphore_signal(barrier, inc=1, device_id=device, device_id_type=MESH)

    first_use = (0, 1, 2, 4, 3, 7, 5, 6)
    wk_copy.start()
    wv_copy.start()
    for b in first_use:
        wq_copy(b).start()
    for b in range(8):
        wo_copy(b).start()

    pl.semaphore_wait(barrier, len(neighbours))

    g = Gather(lambda c, b, dk: xg.at[c, chip(b)], gs, gr, right, left, pair)
    kv = Gather(
        lambda c, b, dk: kvg.at[c, (core + dk) % 2, kv_slot(b)], ks, kr, up, down, beside, other
    )

    x_copies[0].wait()
    g.start_pair(0)
    g.start_ring(0)
    x_copies[1].wait()
    g.start_pair(1)
    wk_across.start()
    wv_across.start()
    for b in first_use:
        wq_across(b).start()
    for b in range(8):
        wo_across(b).start()

    row_id = lax.broadcasted_iota(jnp.int32, (ROWS, ROWS), 0)
    col_id = lax.broadcasted_iota(jnp.int32, (ROWS, ROWS), 1)
    bias[0] = jnp.zeros((ROWS, ROWS), f32)
    bias[1] = jnp.where(col_id <= row_id, 0.0, masked_score).astype(f32)
    bias[2] = jnp.full((ROWS, ROWS), masked_score, f32)
    acc_q[...] = jnp.zeros_like(acc_q)
    acc_kv[...] = jnp.zeros_like(acc_kv)
    ss[...] = jnp.zeros_like(ss)

    even = (lax.broadcasted_iota(jnp.int32, (ROWS, HEAD), 1) % 2) == 0
    low = lax.broadcasted_iota(jnp.int32, (ROWS, HEAD), 1) < 64

    def make_tables():
        lane8 = lax.broadcasted_iota(jnp.int32, (8, HEAD), 1)
        rate8 = jnp.exp2((lane8 // 2).astype(f32) * (-2.0 / HEAD * math.log2(rope_base)))
        rate = jnp.broadcast_to(rate8[:1], (ROWS, HEAD))
        angle = lax.broadcasted_iota(jnp.int32, (ROWS, HEAD), 0).astype(f32) * rate
        cos_r, sin_r = jnp.cos(angle), jnp.sin(angle)
        sign = jnp.where(even, -1.0, 1.0).astype(f32)
        for c in range(2):
            start = (order[2 * cp + c] * ROWS).astype(f32) * rate8
            cos_b, sin_b = jnp.cos(start)[:1], jnp.sin(start)[:1]
            cos_t[c] = cos_b * cos_r - sin_b * sin_r
            sin_t[c] = (sin_b * cos_r + cos_b * sin_r) * sign

    make_tables()

    def project(c, b):
        wide = xg[c, chip(b)].astype(f32)
        square = wide * wide
        ss[c] += square[:, :128] + square[:, 128:256] + square[:, 256:384] + square[:, 384:]
        j = tp_slot(b, 0)
        scaled = jnp.concatenate(
            [
                (wide[:, n * HEAD : (n + 1) * HEAD] * gain[pl.ds(4 * j + n, 1), :]).astype(bf16)
                for n in range(4)
            ],
            axis=1,
        )
        acc_kv[c] += lax.dot_general(
            scaled, wkv[:, features(b, 0)], (((1,), (1,)), ((), ())), preferred_element_type=f32
        )
        for owner in range(2):
            acc_q[c, owner] += jnp.dot(scaled, wq[owner, b], preferred_element_type=f32)

    def partial_copy(c, n):
        if n == 0:
            return to_other(18 + c, part.at[c], part_kv.at[c])
        return to_other(20 + c, acc_q.at[c, 1], part_q.at[c])

    def send_partials(c):
        part[c, :, :HEAD] = acc_kv[c, :, HEAD:]
        part[c, :, HEAD:] = ss[c]
        partial_copy(c, 0).start()
        partial_copy(c, 1).start()

    def turn(y, cosine, sine):
        swapped = jnp.where(even, pltpu.roll(y, HEAD - 1, 1), pltpu.roll(y, 1, 1))
        return y * cosine + swapped * sine

    def finish_kv(c):
        partial_copy(c, 0).wait_recv()
        squares = jnp.sum(ss[c] + part_kv[c, :, HEAD:], axis=1, keepdims=True)
        scale = jnp.broadcast_to(lax.rsqrt(squares * (1.0 / D) + norm_epsilon), (ROWS, HEAD))
        ss[c] = scale
        cosine, sine = cos_t[c], sin_t[c]
        k_cos = jnp.where(core == 0, cosine, pltpu.roll(cosine, 64, 1))
        k_sin = jnp.where(core == 0, sine, pltpu.roll(sine, 64, 1))
        k_cos, k_sin = jnp.where(low, k_cos, 1.0), jnp.where(low, k_sin, 0.0)
        both = (acc_kv[c, :, :HEAD] + part_kv[c, :, :HEAD]) * scale
        kvg[c, core, cp] = turn(both, k_cos, k_sin).astype(bf16)
        kv.start_pair(c)
        kv.start_ring(c)

    def finish_q(c):
        partial_copy(c, 1).wait_recv()
        cosine, sine = cos_t[c], sin_t[c]
        q_scale = ss[c] * (math.log2(math.e) / math.sqrt(HEAD))
        for h in range(4):
            lanes = slice(h * HEAD, (h + 1) * HEAD)
            y = (acc_q[c, 0, :, lanes] + part_q[c, :, lanes]) * q_scale
            q[c, h] = turn(y, cosine, sine).astype(bf16)

    def each(first, last, body):
        def one(i, unused):
            body(i)
            return unused

        lax.fori_loop(first, last, one, 0)

    def when(i, n, action):
        pl.when(i == n)(action)

    def assemble(c, p):
        slot = kv_slot(pick(p, KEY_ORDER))
        lower, upper = kvg[c, 0, slot].astype(f32), kvg[c, 1, slot].astype(f32)
        keys = jnp.where(low, lower, pltpu.roll(upper, 64, 1))
        values = jnp.where(low, pltpu.roll(lower, 64, 1), upper)
        kt[c, p] = keys.T.astype(bf16)
        rows = pl.ds(pl.multiple_of(p * ROWS, ROWS), ROWS)
        v1[c, rows, :HEAD] = values.astype(bf16)
        v1[c, rows, HEAD:] = jnp.ones((ROWS, HEAD), bf16)

    def landed(c, first, last):
        for b in KEY_ORDER[first:last]:
            kv.from_core(c, b)
        each(first, last, functools.partial(assemble, c))

    def unit(qc, kc, start, stop, first, last, between=()):
        q_block = order[2 * cp + qc]
        which = {}
        for p in range(start, stop):
            k_block = order[2 * kv_slot(KEY_ORDER[p]) + kc]
            which[p] = jnp.where(k_block < q_block, 0, jnp.where(k_block == q_block, 1, 2))
        group = 4
        tops = {}

        def score(h, p, best):
            scr = (scr_a, scr_b)[h % 2]
            scores = jnp.dot(q[qc, h], kt[kc, p], preferred_element_type=f32) + bias[which[p]]
            scr[:, p * ROWS : (p + 1) * ROWS] = scores
            here = jnp.maximum(scores[:, :HEAD], scores[:, HEAD:])
            return here if best is None else jnp.maximum(best, here)

        def settle(h, best):
            new_top = jnp.broadcast_to(jnp.max(best, axis=1, keepdims=True), (ROWS, HEAD))
            tops[h] = new_top if first else jnp.maximum(top[qc, h], new_top)

        def weigh(h, p, total):
            scr = (scr_a, scr_b)[h % 2]
            both = jnp.concatenate([tops[h]] * 2, axis=1)
            weights = [
                jnp.exp2(scr[:, n * ROWS : (n + 1) * ROWS] - both).astype(bf16)
                for n in range(p, p + group)
            ]
            here = jnp.dot(
                jnp.concatenate(weights, axis=1),
                v1[kc, p * ROWS : (p + group) * ROWS],
                preferred_element_type=f32,
            )
            return here if total is None else total + here

        def close(h, total):
            if not first:
                shrink = jnp.exp2(top[qc, h] - tops[h])
                total = total + outs[qc, h] * jnp.concatenate([shrink, shrink], axis=1)
            if last:
                sums = total[:, HEAD:]
                att[qc, 0, h] = (total[:, :HEAD] / sums).astype(bf16)
                att_copy(qc, h).start()
                normalizer = (tops[h] + jnp.log2(sums)) * LN2
                norm_out[h : h + 1, qc * ROWS : (qc + 1) * ROWS] = normalizer.T[:1]
            else:
                top[qc, h] = tops[h]
                outs[qc, h] = total

        best = None
        for p in range(start, stop):
            best = score(0, p, best)
        settle(0, best)
        for h in range(4):
            best = total = None
            for p in range(start, stop):
                if h < 3:
                    best = score(h + 1, p, best)
                if p % group == group - 1:
                    total = weigh(h, p - group + 1, total)
            close(h, total)
            if h < 3:
                settle(h + 1, best)
            if h < len(between) and between[h] is not None:
                between[h]()

    def att_copy(c, h):
        return pltpu.make_async_remote_copy(
            src_ref=att.at[c, 0, h],
            dst_ref=att.at[c, 1, h],
            send_sem=ps.at[c * 4 + h],
            recv_sem=pr.at[c * 4 + h],
            device_id=other,
            device_id_type=MESH,
        )

    def rs_copy(c, n, src, dst, device):
        return pltpu.make_async_remote_copy(
            src_ref=src,
            dst_ref=dst,
            send_sem=rs.at[c * 10 + n],
            recv_sem=rr.at[c * 10 + n],
            device_id=device,
            device_id_type=MESH,
        )

    lo, hi = pl.ds(0, HALF), pl.ds(HALF, HALF)
    ways = (right, left)

    def far_pair(c):
        rs_copy(c, 0, terms.at[c, 0], re.at[c], pair).start()

    def far_out(c):
        block = terms.at[c, 1]
        rs_copy(c, 0, re.at[c], re.at[c], pair).wait_recv()
        block[...] = (block[...].astype(f32) + re[c].astype(f32)).astype(bf16)
        rs_copy(c, 1, block.at[lo], ra.at[c], right).start()
        rs_copy(c, 2, block.at[hi], rb.at[c], left).start()

    def near_pair(c, side):
        rs_copy(c, 3 + side, terms.at[c, 2 + side], (rc, rd)[side].at[c, 1], ways[side]).start()

    def near_free(c, side):
        half = (hi, lo)[side]
        rs_copy(
            c, 5 + side, terms.at[c, 4 + side].at[half], (rc, rd)[side].at[c, 0].at[half], ways[side]
        ).start()

    def near_joined(c, side):
        half = (lo, hi)[side]
        block, moved = terms.at[c, 4 + side].at[half], (ra, rb)[side].at[c]
        rs_copy(c, 1 + side, moved, moved, left).wait_recv()
        block[...] = (block[...].astype(f32) + moved[...].astype(f32)).astype(bf16)
        rs_copy(c, 7 + side, block, (rc, rd)[side].at[c, 0].at[half], ways[side]).start()

    def here_in(c, p):
        term = terms[c, 7 - p].astype(f32)
        for side in range(2):
            block = (rc, rd)[side].at[c, p]
            if p == 1:
                rs_copy(c, 3 + side, block, block, left).wait_recv()
            else:
                for n, half in ((5, (hi, lo)[side]), (7, (lo, hi)[side])):
                    rs_copy(c, n + side, block.at[half], block.at[half], left).wait_recv()
            term = term + block[...].astype(f32)
        if p == 1:
            block = terms.at[c, 6]
            block[...] = term.astype(bf16)
            rs_copy(c, 9, block, ry.at[c], pair).start()
        else:
            rs_copy(c, 9, ry.at[c], ry.at[c], pair).wait_recv()
            proj[c * ROWS : (c + 1) * ROWS] = (term + ry[c].astype(f32)).astype(bf16)

    def rs_drain(c):
        whole, half = terms.at[c, 0], terms.at[c, 0, lo]
        for n in range(10):
            ref = half if n in (1, 2, 5, 6, 7, 8) else whole
            rs_copy(c, n, ref, ref, other).wait_send()
        for h in range(4):
            att_copy(c, h).wait_send()

    block_of = {dest: b for b, dest in enumerate((RING[n % 4], n // 4) for n in range(8))}

    def out_products(c):
        for h in range(4):
            att_copy(c, h).wait_recv()
        events = {
            0: lambda: far_pair(c),
            2: lambda: near_pair(c, 0),
            3: lambda: near_pair(c, 1),
        }
        if c == 0:
            events[4] = lambda: near_free(c, 0)
            events[5] = lambda: near_free(c, 1)

        def one(i):
            b = pick(i, [block_of[dest] for dest in DESTS])
            term = None
            for owner in range(2):
                rows = jnp.concatenate([att[c, owner, h] for h in range(4)], axis=1)
                here = jnp.dot(rows, wo[owner, b], preferred_element_type=f32)
                term = here if term is None else term + here
            terms[c, i] = term.astype(bf16)
            for n, action in events.items():
                when(i, n, action)

        each(0, 8, one)

    def gather_event(n):
        if n == 2:
            g.from_sides(0)
        if n == 4:
            g.from_pair(0)
        if n == 5:
            g.from_far(0)
        if n == 6:
            g.pass_on(1)
            g.pass_pair(0)
            g.from_pair(1)
            g.pass_pair(1)
            g.from_sides(1)
        if n == 9:
            g.from_far(1)
        if n == 10:
            g.from_last(0)
        if n == 11:
            g.from_pair_sides(0)
        if n == 13:
            g.from_last(1)
        if n == 14:
            g.from_pair_sides(1)

    def steps(first, last):
        def one(i):
            for n in (2, 4, 5, 6, 9, 10, 11, 13, 14):
                if first <= n < last:
                    when(i, n, functools.partial(gather_event, n))
            code = pick(i - first, [c * 8 + b for c, b in PLAN[first:last]])
            c, b = code // 8, code % 8

            def ready():
                wq_copy(b).wait()
                wq_across(b).wait_recv()

            if any(c == 0 for c, b in PLAN[first:last]):
                pl.when(c == 0)(ready)
            project(c, b)

        each(first, last, one)

    g.pass_on(0)
    g.start_ring(1)
    wk_copy.wait()
    wv_copy.wait()
    wk_across.wait_recv()
    wv_across.wait_recv()
    steps(0, 13)
    send_partials(0)
    finish_kv(0)
    finish_q(0)
    steps(13, 14)
    kv.pass_on(0)
    steps(14, 16)
    send_partials(1)
    kv.from_sides(0)
    kv.from_pair(0)
    kv.pass_pair(0)
    finish_kv(1)
    kv.from_far(0)
    finish_q(1)
    kv.from_pair_sides(0)
    kv.pass_on(1)
    kv.from_last(0)
    kv.from_sides(1)
    kv.from_pair(1)
    kv.pass_pair(1)
    landed(0, 0, 8)
    kv.from_far(1)
    g.drain(0)
    g.drain(1)
    unit(0, 0, 0, 8, True, False, (None, lambda: kv.from_pair_sides(1), None, lambda: kv.from_last(1)))
    landed(1, 0, 4)
    unit(0, 1, 0, 4, False, False)
    landed(1, 4, 8)
    unit(0, 1, 4, 8, False, True)
    for b in range(8):
        wo_copy(b).wait()
        wo_across(b).wait_recv()
    out_products(0)
    unit(1, 0, 0, 8, True, False)
    here_in(0, 1)
    unit(1, 1, 0, 4, False, False)
    unit(1, 1, 4, 8, False, True, (lambda: far_out(0),))
    out_products(1)
    near_joined(0, 0)
    near_joined(0, 1)
    far_out(1)
    near_free(1, 0)
    near_free(1, 1)
    here_in(1, 1)
    here_in(0, 0)
    near_joined(1, 0)
    near_joined(1, 1)
    for b in range(8):
        wq_across(b).wait_send()
        wo_across(b).wait_send()
    wk_across.wait_send()
    wv_across.wait_send()
    for c in range(2):
        partial_copy(c, 0).wait_send()
        partial_copy(c, 1).wait_send()
        kv.drain(c)
    rs_drain(0)
    here_in(1, 0)
    rs_drain(1)


def hand_over(proj, norm, proj_out, norm_out):
    proj_out[...] = proj[...]
    norm_out[...] = norm[...]


def shards(
    checkpoint, norm_gain, query_weight, key_weight, value_weight, output_weight, block_order
):
    vmem = pl.BlockSpec(memory_space=pltpu.VMEM)
    hbm = pl.BlockSpec(memory_space=pl.ANY)
    dma = pltpu.SemaphoreType.DMA
    shapes = (
        jax.ShapeDtypeStruct((2 * ROWS, FEAT), bf16),
        jax.ShapeDtypeStruct((4, 2 * ROWS), f32),
    )
    results = pl.pallas_call(
        kernel,
        out_shape=shapes,
        in_specs=[pl.BlockSpec(memory_space=pltpu.SMEM), hbm, vmem, hbm, hbm, hbm, hbm],
        out_specs=(vmem, vmem),
        scratch_shapes=[
            pltpu.VMEM((2, 8, ROWS, FEAT), bf16),
            pltpu.VMEM((2, 8, FEAT, FEAT), bf16),
            pltpu.VMEM((2 * HEAD, D), bf16),
            pltpu.VMEM((2, 8, FEAT, FEAT), bf16),
            pltpu.VMEM((2, 2, ROWS, FEAT), f32),
            pltpu.VMEM((2, ROWS, 2 * HEAD), f32),
            pltpu.VMEM((2, ROWS, HEAD), f32),
            pltpu.VMEM((2, ROWS, 2 * HEAD), f32),
            pltpu.VMEM((2, ROWS, FEAT), f32),
            pltpu.VMEM((2, ROWS, 2 * HEAD), f32),
            pltpu.VMEM((2, ROWS, HEAD), f32),
            pltpu.VMEM((2, ROWS, HEAD), f32),
            pltpu.VMEM((2, 4, ROWS, HEAD), bf16),
            pltpu.VMEM((2, 2, N_CP, ROWS, HEAD), bf16),
            pltpu.VMEM((2, N_CP, HEAD, ROWS), bf16),
            pltpu.VMEM((2, N_CP * ROWS, 2 * HEAD), bf16),
            pltpu.VMEM((ROWS, N_CP * ROWS), f32),
            pltpu.VMEM((ROWS, N_CP * ROWS), f32),
            pltpu.VMEM((2, 4, ROWS, HEAD), f32),
            pltpu.VMEM((2, 4, ROWS, 2 * HEAD), f32),
            pltpu.VMEM((2, 2, 4, ROWS, HEAD), bf16),
            pltpu.VMEM((3, ROWS, ROWS), f32),
            pltpu.VMEM((2, 8, ROWS, FEAT), bf16),
            pltpu.VMEM((2, HALF, FEAT), bf16),
            pltpu.VMEM((2, HALF, FEAT), bf16),
            pltpu.VMEM((2, 2, ROWS, FEAT), bf16),
            pltpu.VMEM((2, 2, ROWS, FEAT), bf16),
            pltpu.VMEM((2, ROWS, FEAT), bf16),
            pltpu.VMEM((2, ROWS, FEAT), bf16),
            dma((2,)),
            dma((18,)),
            dma((22,)),
            dma((22,)),
            dma((20,)),
            dma((20,)),
            dma((36,)),
            dma((36,)),
            dma((8,)),
            dma((8,)),
            dma((20,)),
            dma((20,)),
        ],
        compiler_params=pltpu.CompilerParams(
            collective_id=0, has_side_effects=True, vmem_limit_bytes=63000000
        ),
        name="sublayer",
    )(
        block_order,
        checkpoint,
        norm_gain.reshape(D // HEAD, HEAD),
        query_weight,
        key_weight.T,
        value_weight.T,
        output_weight,
    )
    return pl.pallas_call(
        hand_over,
        out_shape=shapes,
        in_specs=[vmem, vmem],
        out_specs=(vmem, vmem),
        name="hand_over",
    )(*results)


def solution(mesh):
    return jax.shard_map(
        shards,
        mesh=mesh,
        in_specs=(
            P("cp", "tp"),
            P(),
            P(None, "tp"),
            P(None, "tp"),
            P(None, "tp"),
            P("tp", None),
            P(),
        ),
        out_specs=(P("cp", "tp"), P("tp", "cp")),
        check_vma=False,
    )
```

time: 110 us -> 99.4 us (0.904)
  Pallas kernels: 105 us -> 98.6 us
  local copies, waits for them, and re-layouts: 3.16 us -> 0 us
    pallas_call x1 -> x2, Pallas kernels: 105 us -> 98.6 us  [the longest x1 96.7 us: shards(): pl.pallas_call(kernel, out_shape=shapes, in_specs=[pl.BlockSpec(memory_sp...]
    unnamed x2 -> x0, local copies, waits for them, and re-layouts: 3.16 us -> none
where the time goes in v3:
time: 99.4 us; the launch traced here: 99.2 us
  Pallas kernels  98.6 us (99%)
    pallas_call x1, Pallas kernels, shards(): pl.pallas_call(kernel, out_shape=shapes, in_specs=[pl.BlockSpec(memory_sp...  96.7 us

profile of v3, /device:TPU:1, one launch (start us, length us, event | category | flops | bytes accessed | tf_op | source)
XLA Modules:
  0.0 99.2 jit_solution(671462096968906780)
XLA Ops:
  0.6 96.7 %sublayer.1 = (bf16[512,512]{1,0:T(8,128)(2,1)}, f32[4,512]{1,0:T(4,128)}) custom-call(s32[16]{0:T(128)} %order.1, bf16[512,512]{1,0:T(8,128)(2,1)} %x_hbm.1, f32[64,128]{1,0:T(8,128)} %bitcast.5, bf16[8192,512]{1,0:T(8,128)(2,1)} %wq_hbm.1, bf16[64,8192]{1,0:T(8,128)(2,1)} %bitcast.3, bf16[64,8192]{1,0:T(8,128)(2,1)} %bitcast.4, bf16[512,8192]{1,0:T(8,128)(2,1)} %wo_hbm.1), custom_call_target="tpu_custom_call" | custom-call | tf_op jit(solution)/shard_map/sublayer/pallas_call | solution.py:627
  97.3 1.9 %hand_over.1 = (bf16[512,512]{1,0:T(8,128)(2,1)}, f32[4,512]{1,0:T(4,128)}) custom-call(bf16[512,512]{1,0:T(8,128)(2,1)} %get-tuple-element.4.proj, f32[4,512]{1,0:T(4,128)} %get-tuple-element.5.norm), custom_call_target="tpu_custom_call" | custom-call | tf_op jit(solution)/shard_map/hand_over/pallas_call | solution.py:688

commit v4 on v3

--- a/solution.py
+++ b/solution.py
@@ -60,12 +60,13 @@
         self.copy(c, 8, self.ref(c, 0), self.pair).start()
         self.send_core(c, 0)
 
-    def start_ring(self, c):
-        lower, upper = self.ref(c, 0, rows=0), self.ref(c, 0, rows=1)
-        self.copy(c, 0, lower, self.right).start()
-        self.copy(c, 4, upper, self.left).start()
-        self.copy(c, 1, upper, self.right).start()
-        self.copy(c, 5, lower, self.left).start()
+    def start_first(self, c):
+        self.copy(c, 0, self.ref(c, 0, rows=0), self.right).start()
+        self.copy(c, 4, self.ref(c, 0, rows=1), self.left).start()
+
+    def start_second(self, c):
+        self.copy(c, 1, self.ref(c, 0, rows=1), self.right).start()
+        self.copy(c, 5, self.ref(c, 0, rows=0), self.left).start()
 
     def pass_on(self, c):
         block = self.ref(c, 1, rows=0)
@@ -117,10 +118,10 @@
 
 RING = (0, 3, 1, 2)
 KEY_ORDER = (0, 1, 2, 4, 3, 5, 6, 7)
-DESTS = ((2, 1), (2, 0), (1, 1), (3, 1), (1, 0), (3, 0), (0, 1), (0, 0))
+DESTS = ((1, 1), (3, 1), (2, 1), (1, 0), (3, 0), (2, 0), (0, 1), (0, 0))
 PLAN = (
-    (0, 0), (1, 0), (0, 1), (0, 2), (0, 4), (0, 3), (1, 1), (1, 2),
-    (1, 4), (1, 3), (0, 7), (0, 5), (0, 6), (1, 7), (1, 5), (1, 6),
+    (0, 0), (1, 0), (0, 1), (0, 2), (0, 4), (0, 3), (1, 4), (0, 7), (0, 5), (0, 6),
+    (1, 3), (1, 1), (1, 2), (1, 7),
 )
 
 
@@ -215,7 +216,8 @@
 
     x_copies[0].wait()
     g.start_pair(0)
-    g.start_ring(0)
+    g.start_first(0)
+    g.start_second(0)
     x_copies[1].wait()
     g.start_pair(1)
     wk_across.start()
@@ -252,23 +254,30 @@
 
     make_tables()
 
-    def project(c, b):
+    def scaled_block(c, b):
         wide = xg[c, chip(b)].astype(f32)
+        j = tp_slot(b, 0)
+        pieces = [
+            (wide[:, n * HEAD : (n + 1) * HEAD] * gain[pl.ds(4 * j + n, 1), :]).astype(bf16)
+            for n in range(4)
+        ]
+        return wide, jnp.concatenate(pieces, axis=1)
+
+    def project_kv(c, b, wide, scaled):
         square = wide * wide
         ss[c] += square[:, :128] + square[:, 128:256] + square[:, 256:384] + square[:, 384:]
-        j = tp_slot(b, 0)
-        scaled = jnp.concatenate(
-            [
-                (wide[:, n * HEAD : (n + 1) * HEAD] * gain[pl.ds(4 * j + n, 1), :]).astype(bf16)
-                for n in range(4)
-            ],
-            axis=1,
-        )
         acc_kv[c] += lax.dot_general(
             scaled, wkv[:, features(b, 0)], (((1,), (1,)), ((), ())), preferred_element_type=f32
         )
+
+    def project_q(c, b, scaled):
         for owner in range(2):
             acc_q[c, owner] += jnp.dot(scaled, wq[owner, b], preferred_element_type=f32)
+
+    def project(c, b):
+        wide, scaled = scaled_block(c, b)
+        project_kv(c, b, wide, scaled)
+        project_q(c, b, scaled)
 
     def partial_copy(c, n):
         if n == 0:
@@ -279,7 +288,6 @@
         part[c, :, :HEAD] = acc_kv[c, :, HEAD:]
         part[c, :, HEAD:] = ss[c]
         partial_copy(c, 0).start()
-        partial_copy(c, 1).start()
 
     def turn(y, cosine, sine):
         swapped = jnp.where(even, pltpu.roll(y, HEAD - 1, 1), pltpu.roll(y, 1, 1))
@@ -297,7 +305,8 @@
         both = (acc_kv[c, :, :HEAD] + part_kv[c, :, :HEAD]) * scale
         kvg[c, core, cp] = turn(both, k_cos, k_sin).astype(bf16)
         kv.start_pair(c)
-        kv.start_ring(c)
+        kv.start_first(c)
+        kv.start_second(c)
 
     def finish_q(c):
         partial_copy(c, 1).wait_recv()
@@ -422,27 +431,27 @@
     ways = (right, left)
 
     def far_pair(c):
-        rs_copy(c, 0, terms.at[c, 0], re.at[c], pair).start()
+        rs_copy(c, 0, terms.at[c, 2], re.at[c], pair).start()
 
     def far_out(c):
-        block = terms.at[c, 1]
+        block = terms.at[c, 5]
         rs_copy(c, 0, re.at[c], re.at[c], pair).wait_recv()
         block[...] = (block[...].astype(f32) + re[c].astype(f32)).astype(bf16)
         rs_copy(c, 1, block.at[lo], ra.at[c], right).start()
         rs_copy(c, 2, block.at[hi], rb.at[c], left).start()
 
     def near_pair(c, side):
-        rs_copy(c, 3 + side, terms.at[c, 2 + side], (rc, rd)[side].at[c, 1], ways[side]).start()
+        rs_copy(c, 3 + side, terms.at[c, side], (rc, rd)[side].at[c, 1], ways[side]).start()
 
     def near_free(c, side):
         half = (hi, lo)[side]
         rs_copy(
-            c, 5 + side, terms.at[c, 4 + side].at[half], (rc, rd)[side].at[c, 0].at[half], ways[side]
+            c, 5 + side, terms.at[c, 3 + side].at[half], (rc, rd)[side].at[c, 0].at[half], ways[side]
         ).start()
 
     def near_joined(c, side):
         half = (lo, hi)[side]
-        block, moved = terms.at[c, 4 + side].at[half], (ra, rb)[side].at[c]
+        block, moved = terms.at[c, 3 + side].at[half], (ra, rb)[side].at[c]
         rs_copy(c, 1 + side, moved, moved, left).wait_recv()
         block[...] = (block[...].astype(f32) + moved[...].astype(f32)).astype(bf16)
         rs_copy(c, 7 + side, block, (rc, rd)[side].at[c, 0].at[half], ways[side]).start()
@@ -479,13 +488,13 @@
         for h in range(4):
             att_copy(c, h).wait_recv()
         events = {
-            0: lambda: far_pair(c),
-            2: lambda: near_pair(c, 0),
-            3: lambda: near_pair(c, 1),
+            0: lambda: near_pair(c, 0),
+            1: lambda: near_pair(c, 1),
+            2: lambda: far_pair(c),
         }
         if c == 0:
-            events[4] = lambda: near_free(c, 0)
-            events[5] = lambda: near_free(c, 1)
+            events[3] = lambda: near_free(c, 0)
+            events[4] = lambda: near_free(c, 1)
 
         def one(i):
             b = pick(i, [block_of[dest] for dest in DESTS])
@@ -505,28 +514,32 @@
             g.from_sides(0)
         if n == 4:
             g.from_pair(0)
+            g.pass_pair(0)
         if n == 5:
             g.from_far(0)
         if n == 6:
             g.pass_on(1)
-            g.pass_pair(0)
+            g.start_second(1)
             g.from_pair(1)
             g.pass_pair(1)
+        if n == 7:
+            g.from_last(0)
+        if n == 8:
+            g.from_pair_sides(0)
+        if n == 11:
+            kv.pass_on(0)
             g.from_sides(1)
-        if n == 9:
-            g.from_far(1)
-        if n == 10:
-            g.from_last(0)
-        if n == 11:
-            g.from_pair_sides(0)
         if n == 13:
+            kv.from_sides(0)
+            kv.from_pair(0)
+            kv.pass_pair(0)
+            kv.from_far(0)
+            kv.from_pair_sides(0)
             g.from_last(1)
-        if n == 14:
-            g.from_pair_sides(1)
 
     def steps(first, last):
         def one(i):
-            for n in (2, 4, 5, 6, 9, 10, 11, 13, 14):
+            for n in (2, 4, 5, 6, 7, 8, 11, 13):
                 if first <= n < last:
                     when(i, n, functools.partial(gather_event, n))
             code = pick(i - first, [c * 8 + b for c, b in PLAN[first:last]])
@@ -543,38 +556,44 @@
         each(first, last, one)
 
     g.pass_on(0)
-    g.start_ring(1)
+    g.start_first(1)
     wk_copy.wait()
     wv_copy.wait()
     wk_across.wait_recv()
     wv_across.wait_recv()
-    steps(0, 13)
+    steps(0, 10)
     send_partials(0)
+    partial_copy(0, 1).start()
     finish_kv(0)
+    g.from_far(1)
     finish_q(0)
-    steps(13, 14)
-    kv.pass_on(0)
-    steps(14, 16)
+    steps(10, 14)
+    kv.from_last(0)
+    landed(0, 0, 4)
+    g.from_pair_sides(1)
+    late = [scaled_block(1, b) for b in (5, 6)]
+    for b, (wide, scaled) in zip((5, 6), late):
+        project_kv(1, b, wide, scaled)
     send_partials(1)
-    kv.from_sides(0)
-    kv.from_pair(0)
-    kv.pass_pair(0)
+    for b, (wide, scaled) in zip((5, 6), late):
+        project_q(1, b, scaled)
+    partial_copy(1, 1).start()
     finish_kv(1)
-    kv.from_far(0)
+    landed(0, 4, 8)
     finish_q(1)
-    kv.from_pair_sides(0)
-    kv.pass_on(1)
-    kv.from_last(0)
-    kv.from_sides(1)
-    kv.from_pair(1)
-    kv.pass_pair(1)
-    landed(0, 0, 8)
-    kv.from_far(1)
     g.drain(0)
     g.drain(1)
-    unit(0, 0, 0, 8, True, False, (None, lambda: kv.from_pair_sides(1), None, lambda: kv.from_last(1)))
+
+    def near_keys():
+        kv.from_sides(1)
+        kv.from_pair(1)
+        kv.pass_pair(1)
+
+    unit(0, 0, 0, 8, True, False, (lambda: kv.pass_on(1), near_keys))
+    kv.from_far(1)
     landed(1, 0, 4)
-    unit(0, 1, 0, 4, False, False)
+    unit(0, 1, 0, 4, False, False, (None, None, lambda: kv.from_pair_sides(1)))
+    kv.from_last(1)
     landed(1, 4, 8)
     unit(0, 1, 4, 8, False, True)
     for b in range(8):
@@ -582,10 +601,10 @@
         wo_across(b).wait_recv()
     out_products(0)
     unit(1, 0, 0, 8, True, False)
-    here_in(0, 1)
     unit(1, 1, 0, 4, False, False)
     unit(1, 1, 4, 8, False, True, (lambda: far_out(0),))
     out_products(1)
+    here_in(0, 1)
     near_joined(0, 0)
     near_joined(0, 1)
     far_out(1)

time: 99.4 us -> 95.5 us (0.961)
  Pallas kernels: 98.6 us -> 94.6 us
    pallas_call x1, Pallas kernels: 96.7 us -> 92.8 us  [shards(): pl.pallas_call(kernel, out_shape=shapes, in_specs=[pl.BlockSpec(memory_sp...]
where the time goes in v4:
time: 95.5 us; the launch traced here: 95.3 us
  Pallas kernels  94.6 us (99%)
    pallas_call x1, Pallas kernels, shards(): pl.pallas_call(kernel, out_shape=shapes, in_specs=[pl.BlockSpec(memory_sp...  92.8 us

profile of v4, /device:TPU:1, one launch (start us, length us, event | category | flops | bytes accessed | tf_op | source)
XLA Modules:
  0.0 95.3 jit_solution(14473587903340443514)
XLA Ops:
  0.6 92.8 %sublayer.1 = (bf16[512,512]{1,0:T(8,128)(2,1)}, f32[4,512]{1,0:T(4,128)}) custom-call(s32[16]{0:T(128)} %order.1, bf16[512,512]{1,0:T(8,128)(2,1)} %x_hbm.1, f32[64,128]{1,0:T(8,128)} %bitcast.5, bf16[8192,512]{1,0:T(8,128)(2,1)} %wq_hbm.1, bf16[64,8192]{1,0:T(8,128)(2,1)} %bitcast.3, bf16[64,8192]{1,0:T(8,128)(2,1)} %bitcast.4, bf16[512,8192]{1,0:T(8,128)(2,1)} %wo_hbm.1), custom_call_target="tpu_custom_call" | custom-call | tf_op jit(solution)/shard_map/sublayer/pallas_call | solution.py:646
  93.4 1.9 %hand_over.1 = (bf16[512,512]{1,0:T(8,128)(2,1)}, f32[4,512]{1,0:T(4,128)}) custom-call(bf16[512,512]{1,0:T(8,128)(2,1)} %get-tuple-element.4.proj, f32[4,512]{1,0:T(4,128)} %get-tuple-element.5.norm), custom_call_target="tpu_custom_call" | custom-call | tf_op jit(solution)/shard_map/hand_over/pallas_call | solution.py:707

commit v5 on v4

--- a/solution.py
+++ b/solution.py
@@ -128,7 +128,7 @@
 def kernel(
     order, x_hbm, gain, wq_hbm, wk_hbm, wv_hbm, wo_hbm,
     proj, norm_out,
-    xg, wq, wkv, wo, acc_q, acc_kv, ss, part, part_q, part_kv, cos_t, sin_t, q, kvg, kt, v1,
+    xg, wq, wkv, wo, acc_q, acc_kv, ss, part, part_q, part_kv, cos_t, sin_t, q, kvg,
     scr_a, scr_b, top, outs, att, bias, terms, ra, rb, rc, rd, re, ry,
     x_sem, w_sem, xs, xr, gs, gr, ks, kr, ps, pr, rs, rr,
 ):
@@ -189,10 +189,12 @@
     def wo_across(b):
         return to_other(8 + b, wo_hbm.at[:, features(b, 1)], wo.at[1, b])
 
-    wk_copy = pltpu.make_async_copy(wk_hbm, wkv.at[pl.ds(0, 64)], w_sem.at[16])
-    wv_copy = pltpu.make_async_copy(wv_hbm, wkv.at[pl.ds(64, 64)], w_sem.at[17])
-    wk_across = to_other(16, wk_hbm, wkv.at[pl.ds(128, 64)])
-    wv_across = to_other(17, wv_hbm, wkv.at[pl.ds(192, 64)])
+    outer = pl.ds(pl.multiple_of(192 * core, 64), 64)
+    inner = pl.ds(pl.multiple_of(128 - 64 * core, 64), 64)
+    wk_copy = pltpu.make_async_copy(wk_hbm, wkv.at[outer], w_sem.at[16])
+    wv_copy = pltpu.make_async_copy(wv_hbm, wkv.at[inner], w_sem.at[17])
+    wk_across = to_other(16, wk_hbm, wkv.at[inner])
+    wv_across = to_other(17, wv_hbm, wkv.at[outer])
 
     barrier = pltpu.get_barrier_semaphore()
     neighbours = (right, left, pair, other, up, down, beside)
@@ -237,7 +239,6 @@
     ss[...] = jnp.zeros_like(ss)
 
     even = (lax.broadcasted_iota(jnp.int32, (ROWS, HEAD), 1) % 2) == 0
-    low = lax.broadcasted_iota(jnp.int32, (ROWS, HEAD), 1) < 64
 
     def make_tables():
         lane8 = lax.broadcasted_iota(jnp.int32, (8, HEAD), 1)
@@ -299,11 +300,10 @@
         scale = jnp.broadcast_to(lax.rsqrt(squares * (1.0 / D) + norm_epsilon), (ROWS, HEAD))
         ss[c] = scale
         cosine, sine = cos_t[c], sin_t[c]
-        k_cos = jnp.where(core == 0, cosine, pltpu.roll(cosine, 64, 1))
-        k_sin = jnp.where(core == 0, sine, pltpu.roll(sine, 64, 1))
-        k_cos, k_sin = jnp.where(low, k_cos, 1.0), jnp.where(low, k_sin, 0.0)
         both = (acc_kv[c, :, :HEAD] + part_kv[c, :, :HEAD]) * scale
-        kvg[c, core, cp] = turn(both, k_cos, k_sin).astype(bf16)
+        turned = turn(both, cosine, sine)
+        keys = jnp.concatenate([turned[:HALF].T, turned[HALF:].T], axis=0)
+        kvg[c, core, cp] = jnp.where(core == 0, keys, both).astype(bf16)
         kv.start_pair(c)
         kv.start_first(c)
         kv.start_second(c)
@@ -327,33 +327,25 @@
     def when(i, n, action):
         pl.when(i == n)(action)
 
-    def assemble(c, p):
-        slot = kv_slot(pick(p, KEY_ORDER))
-        lower, upper = kvg[c, 0, slot].astype(f32), kvg[c, 1, slot].astype(f32)
-        keys = jnp.where(low, lower, pltpu.roll(upper, 64, 1))
-        values = jnp.where(low, pltpu.roll(lower, 64, 1), upper)
-        kt[c, p] = keys.T.astype(bf16)
-        rows = pl.ds(pl.multiple_of(p * ROWS, ROWS), ROWS)
-        v1[c, rows, :HEAD] = values.astype(bf16)
-        v1[c, rows, HEAD:] = jnp.ones((ROWS, HEAD), bf16)
-
     def landed(c, first, last):
         for b in KEY_ORDER[first:last]:
             kv.from_core(c, b)
-        each(first, last, functools.partial(assemble, c))
 
     def unit(qc, kc, start, stop, first, last, between=()):
         q_block = order[2 * cp + qc]
-        which = {}
+        which, slots = {}, {}
         for p in range(start, stop):
-            k_block = order[2 * kv_slot(KEY_ORDER[p]) + kc]
+            slots[p] = kv_slot(KEY_ORDER[p])
+            k_block = order[2 * slots[p] + kc]
             which[p] = jnp.where(k_block < q_block, 0, jnp.where(k_block == q_block, 1, 2))
         group = 4
         tops = {}
 
         def score(h, p, best):
             scr = (scr_a, scr_b)[h % 2]
-            scores = jnp.dot(q[qc, h], kt[kc, p], preferred_element_type=f32) + bias[which[p]]
+            halves = [kvg[kc, 0, slots[p], :HALF], kvg[kc, 0, slots[p], HALF:]]
+            keys = jnp.concatenate(halves, axis=1)
+            scores = jnp.dot(q[qc, h], keys, preferred_element_type=f32) + bias[which[p]]
             scr[:, p * ROWS : (p + 1) * ROWS] = scores
             here = jnp.maximum(scores[:, :HEAD], scores[:, HEAD:])
             return here if best is None else jnp.maximum(best, here)
@@ -369,9 +361,10 @@
                 jnp.exp2(scr[:, n * ROWS : (n + 1) * ROWS] - both).astype(bf16)
                 for n in range(p, p + group)
             ]
+            values = jnp.concatenate([kvg[kc, 1, slots[n]] for n in range(p, p + group)], axis=0)
             here = jnp.dot(
                 jnp.concatenate(weights, axis=1),
-                v1[kc, p * ROWS : (p + group) * ROWS],
+                jnp.concatenate([values, jnp.ones((group * ROWS, HEAD), bf16)], axis=1),
                 preferred_element_type=f32,
             )
             return here if total is None else total + here
@@ -663,8 +656,6 @@
             pltpu.VMEM((2, ROWS, HEAD), f32),
             pltpu.VMEM((2, 4, ROWS, HEAD), bf16),
             pltpu.VMEM((2, 2, N_CP, ROWS, HEAD), bf16),
-            pltpu.VMEM((2, N_CP, HEAD, ROWS), bf16),
-            pltpu.VMEM((2, N_CP * ROWS, 2 * HEAD), bf16),
             pltpu.VMEM((ROWS, N_CP * ROWS), f32),
             pltpu.VMEM((ROWS, N_CP * ROWS), f32),
             pltpu.VMEM((2, 4, ROWS, HEAD), f32),

time: 95.5 us -> 94 us (0.984)
  Pallas kernels: 94.6 us -> 93.2 us
    pallas_call x1, Pallas kernels: 92.8 us -> 91.3 us  [shards(): pl.pallas_call(kernel, out_shape=shapes, in_specs=[pl.BlockSpec(memory_sp...]
where the time goes in v5:
time: 94 us; the launch traced here: 93.8 us
  Pallas kernels  93.2 us (99%)
    pallas_call x1, Pallas kernels, shards(): pl.pallas_call(kernel, out_shape=shapes, in_specs=[pl.BlockSpec(memory_sp...  91.3 us

profile of v5, /device:TPU:1, one launch (start us, length us, event | category | flops | bytes accessed | tf_op | source)
XLA Modules:
  0.0 93.8 jit_solution(16771687895899820705)
XLA Ops:
  0.6 91.3 %sublayer.1 = (bf16[512,512]{1,0:T(8,128)(2,1)}, f32[4,512]{1,0:T(4,128)}) custom-call(s32[16]{0:T(128)} %order.1, bf16[512,512]{1,0:T(8,128)(2,1)} %x_hbm.1, f32[64,128]{1,0:T(8,128)} %bitcast.5, bf16[8192,512]{1,0:T(8,128)(2,1)} %wq_hbm.1, bf16[64,8192]{1,0:T(8,128)(2,1)} %bitcast.3, bf16[64,8192]{1,0:T(8,128)(2,1)} %bitcast.4, bf16[512,8192]{1,0:T(8,128)(2,1)} %wo_hbm.1), custom_call_target="tpu_custom_call" | custom-call | tf_op jit(solution)/shard_map/sublayer/pallas_call | solution.py:639
  91.9 1.9 %hand_over.1 = (bf16[512,512]{1,0:T(8,128)(2,1)}, f32[4,512]{1,0:T(4,128)}) custom-call(bf16[512,512]{1,0:T(8,128)(2,1)} %get-tuple-element.4.proj, f32[4,512]{1,0:T(4,128)} %get-tuple-element.5.norm), custom_call_target="tpu_custom_call" | custom-call | tf_op jit(solution)/shard_map/hand_over/pallas_call | solution.py:698

commit v6 on v5

--- a/solution.py
+++ b/solution.py
@@ -638,7 +638,7 @@
     )
     results = pl.pallas_call(
         kernel,
-        out_shape=shapes,
+        out_shape=tuple(pltpu.VMEM(shape.shape, shape.dtype) for shape in shapes),
         in_specs=[pl.BlockSpec(memory_space=pltpu.SMEM), hbm, vmem, hbm, hbm, hbm, hbm],
         out_specs=(vmem, vmem),
         scratch_shapes=[
@@ -701,7 +701,7 @@
         in_specs=[vmem, vmem],
         out_specs=(vmem, vmem),
         name="hand_over",
-    )(*results)
+    )(*(pltpu.with_memory_space_constraint(result, pltpu.VMEM) for result in results))
 
 
 def solution(mesh):

time: 94 us -> 92.1 us (0.980)
  Pallas kernels: 93.2 us -> 91.3 us
    pallas_call x1, Pallas kernels: 1.87 us -> 0.83 us  [shards(): pl.pallas_call(hand_over, out_shape=shapes, in_specs=[vmem, vmem], out_sp...]
where the time goes in v6:
time: 92.1 us; the launch traced here: 92 us
  Pallas kernels  91.3 us (99%)
    pallas_call x1, Pallas kernels, shards(): pl.pallas_call(kernel, out_shape=tuple((pltpu.VMEM(shape.shape, shape.dty...  90.5 us

profile of v6, /device:TPU:1, one launch (start us, length us, event | category | flops | bytes accessed | tf_op | source)
XLA Modules:
  0.0 92.0 jit_solution(4594494871160963176)
XLA Ops:
  0.6 90.5 %sublayer.1 = (bf16[512,512]{1,0:T(8,128)(2,1)S(1)}, f32[4,512]{1,0:T(4,128)S(1)}) custom-call(s32[16]{0:T(128)} %order.1, bf16[512,512]{1,0:T(8,128)(2,1)} %x_hbm.1, f32[64,128]{1,0:T(8,128)} %bitcast.5, bf16[8192,512]{1,0:T(8,128)(2,1)} %wq_hbm.1, bf16[64,8192]{1,0:T(8,128)(2,1)} %bitcast.3, bf16[64,8192]{1,0:T(8,128)(2,1)} %bitcast.4, ...), custom_call_target="tpu_custom_call" | custom-call | tf_op jit(solution)/shard_map/sublayer/pallas_call | solution.py:639
  91.1 0.8 hand_over.1

commit v7 on v6

--- a/solution.py
+++ b/solution.py
@@ -478,8 +478,10 @@
     block_of = {dest: b for b, dest in enumerate((RING[n % 4], n // 4) for n in range(8))}
 
     def out_products(c):
-        for h in range(4):
-            att_copy(c, h).wait_recv()
+        def partner():
+            for h in range(4):
+                att_copy(c, h).wait_recv()
+
         events = {
             0: lambda: near_pair(c, 0),
             1: lambda: near_pair(c, 1),
@@ -495,6 +497,8 @@
             for owner in range(2):
                 rows = jnp.concatenate([att[c, owner, h] for h in range(4)], axis=1)
                 here = jnp.dot(rows, wo[owner, b], preferred_element_type=f32)
+                if term is None:
+                    when(i, 0, partner)
                 term = here if term is None else term + here
             terms[c, i] = term.astype(bf16)
             for n, action in events.items():

time: 92.1 us -> 92.4 us (level)
  no operation moved by 1% of the time
where the time goes in v7:
time: 92.4 us; the launch traced here: 92.3 us
  Pallas kernels  91.6 us (99%)
    pallas_call x1, Pallas kernels, shards(): pl.pallas_call(kernel, out_shape=tuple((pltpu.VMEM(shape.shape, shape.dty...  90.8 us

profile of v7, /device:TPU:1, one launch (start us, length us, event | category | flops | bytes accessed | tf_op | source)
XLA Modules:
  0.0 92.3 jit_solution(2803723388598918914)
XLA Ops:
  0.6 90.8 %sublayer.1 = (bf16[512,512]{1,0:T(8,128)(2,1)S(1)}, f32[4,512]{1,0:T(4,128)S(1)}) custom-call(s32[16]{0:T(128)} %order.1, bf16[512,512]{1,0:T(8,128)(2,1)} %x_hbm.1, f32[64,128]{1,0:T(8,128)} %bitcast.5, bf16[8192,512]{1,0:T(8,128)(2,1)} %wq_hbm.1, bf16[64,8192]{1,0:T(8,128)(2,1)} %bitcast.3, bf16[64,8192]{1,0:T(8,128)(2,1)} %bitcast.4, ...), custom_call_target="tpu_custom_call" | custom-call | tf_op jit(solution)/shard_map/sublayer/pallas_call | solution.py:643
  91.4 0.8 hand_over.1
